TPU v7x, 32 devices: a whole 2x2x4 slice. The times are simulated.
32 devices in a mesh: blk: 4 (over x, core), vox: 8 (over z, y).
Axes of the slice: x: 2, y: 2, z: 4, core: 2. Of those that a mesh axis runs over, the one named last changes fastest.
Arguments:
- src_fields: bfloat16 [256, 32768], P('blk', 'vox'), may hold values from -6 to 6
- det_fields: bfloat16 [256, 32768], P('blk', 'vox'), may hold values from -6 to 6
- probes: bfloat16 [2, 32768], P(None, 'vox'), may hold values from -6 to 6
Outputs:
- curvature: float32 [2, 32768], P(None, 'vox')
All inputs are finite; a program needn't handle non-finite values.
Results may differ from a plain program's by a relative error of at most 0.0016.
Values may be sent and summed in bfloat16 or wider, within the bound.
No kernel may reach another device: no remote copies, remote signals or barrier semaphores. Data moves between devices by JAX's collectives and lax.ppermute only.
A program may use at most 64 MiB of HBM per device.

v0:
```python
import jax
import jax.numpy as jnp
from jax import lax
from jax.sharding import PartitionSpec as P


def shards(src_fields, det_fields, probes):
    src_count, vox_count = src_fields.shape
    det_count = det_fields.shape[0]
    groups = lax.axis_size("blk")
    det_total = det_count * groups
    probe_count = probes.shape[0]
    weighted = (src_fields.astype(jnp.float32)[None] * probes.astype(jnp.float32)[:, None]).astype(
        jnp.bfloat16
    )
    weighted = weighted.reshape(probe_count * src_count, vox_count)
    slab = jnp.zeros((0, vox_count), jnp.bfloat16)
    product = jnp.einsum(
        "rv,dv->rd",
        weighted,
        lax.all_gather(det_fields, "blk", axis=0, tiled=True),
        preferred_element_type=jnp.float32,
    )
    partial_value, slab = (product, slab)
    measured = lax.psum(partial_value, "vox")
    measured_b = measured.astype(jnp.bfloat16)
    backproj = jnp.dot(
        measured_b,
        lax.all_gather(det_fields, "blk", axis=0, tiled=True),
        preferred_element_type=jnp.float32,
    )
    backproj = backproj.reshape(probe_count, src_count, vox_count)
    contrib = jnp.sum(src_fields.astype(jnp.float32)[None] * backproj, axis=1)
    total = lax.psum(contrib, "blk")
    normalizer = jnp.float32(1.0 / (src_count * groups * det_total))
    return total * normalizer


def solution(mesh):
    return jax.shard_map(
        shards,
        mesh=mesh,
        in_specs=(P("blk", "vox"), P("blk", "vox"), P(None, "vox")),
        out_specs=P(None, "vox"),
        check_vma=False,
    )
```

profile of v0, /device:TPU:0, one launch (start us, length us, event | category | flops | bytes accessed | tf_op | source)
XLA Modules:
  0.0 93.9 jit_solution(10206651195195280861)
XLA Ops:
  6.5 0.0 all-gather.2.cloned.1.call-start
  6.5 0.7 all-gather.2.cloned.1.call-update
  7.3 0.7 convert_element_type.18
  8.0 1.1 %convert_element_type.17 = f32[64,4096]{1,0:T(8,128)S(1)} convert(bf16[64,4096]{1,0:T(8,128)(2,1)} %param.3) | non-fusion elementwise | flops 262144 | bytes 1572864 | tf_op jit(solution)/shard_map/convert_element_type | solution.py:33
  9.1 1.1 %multiply_convert_fusion = bf16[2,64,4096]{2,1,0:T(8,128)(2,1)} fusion(f32[2,4096]{1,0:T(2,128)S(1)} %convert_element_type.18, f32[64,4096]{1,0:T(8,128)S(1)} %convert_element_type.17), kind=kLoop, calls=%fused_computation.1 | loop fusion | flops 1048576 | bytes 2129920 | tf_op jit(solution)/shard_map/convert_element_type | solution.py:13
  10.3 24.0 %all-gather.2.cloned.1.call-done = bf16[256,4096]{1,0:T(8,128)(2,1)} async-done(((bf16[64,4096]{1,0:T(8,128)(2,1)}), bf16[256,4096]{1,0:T(8,128)(2,1)}) %all-gather.2.cloned.1.call-update) | async-done | bytes 2097168 | tf_op jit(solution)/shard_map/all_gather | solution.py:21
  34.2 0.0 copy-start
  34.2 2.9 %fusion.2 = f32[128,256]{1,0:T(8,128)S(1)} fusion(bf16[128,4096]{1,0:T(8,128)(2,1)} %bitcast.7, bf16[256,4096]{1,0:T(8,128)(2,1)} %all-gather.2.cloned.1.call-done), kind=kOutput, calls=%fused_computation.5 | convolution fusion | flops 268435456 | bytes 3276800 | tf_op jit(solution)/shard_map/rv,dv->rd/dot_general | solution.py:18
  37.1 38.3 %all-reduce.1 = bf16[128,256]{1,0:T(8,128)(2,1)S(1)} all-reduce(f32[128,256]{1,0:T(8,128)S(1)} %fusion.2), channel_id=1, replica_groups=mesh['blk'=4,'vox'=8] {'vox'}, use_global_device_ids=true, to_apply=%region_0.0 | all-reduce | flops 32768 | bytes 196608 | tf_op jit(solution)/shard_map/psum | solution.py:25
  75.5 0.0 copy-done
  75.5 0.5 multiply_reduce_fusion
  76.0 10.4 %psum.15 = f32[2,4096]{1,0:T(2,128)S(1)} all-reduce(f32[2,4096]{1,0:T(2,128)S(1)} %multiply_reduce_fusion), channel_id=1, replica_groups=mesh['blk'=4,'vox'=8] {'blk'}, use_global_device_ids=true, to_apply=%region_2.0 | all-reduce | flops 8192 | bytes 65536 | tf_op jit(solution)/shard_map/psum | solution.py:34
  86.4 0.6 broadcast_multiply_fusion
Async XLA Ops:
  6.5 27.7 %all-gather.2.cloned.1.call-start = ((), (), s32[]{:S(2)}) async-start(), calls=%async_computation | async-start | bytes 2621440 | tf_op jit(solution)/shard_map/all_gather | solution.py:21
  34.2 41.2 %copy-start = (bf16[256,4096]{1,0:T(8,128)(2,1)S(1)}, bf16[256,4096]{1,0:T(8,128)(2,1)}, u32[]{:S(2)}) copy-start(bf16[256,4096]{1,0:T(8,128)(2,1)} %all-gather.2.cloned.1.call-done) | copy-start | bytes 6291460
Sparse Core Ops, SparseCore 0:
  8.9 25.2 all-gather.1
where the time goes:
time: 94.1 us; the launch traced here: 93.9 us
  blocking collectives  48.8 us (52%)
  waiting for transfers between devices  24.7 us (26%)
  between operations  13.4 us (14%)
  other arithmetic  3.62 us (4%)
  matrix products  3.39 us (4%)
    psum x1, blocking collectives, shards(): measured = lax.psum(partial_value, 'vox')  38.3 us
    all_gather x1, waiting for transfers between devices, shards(): lax.all_gather(det_fields, 'blk', axis=0, tiled=True)  24 us
    psum x1, blocking collectives, shards(): total = lax.psum(contrib, 'blk')  10.4 us
    dot_general x1, matrix products, shards(): jnp.einsum('rv,dv->rd', weighted, lax.all_gather(det_fields, 'blk', axis=...  2.89 us
  transfers between devices with their start and end apart: 1, of which 1 were waited for; matrix products, arithmetic and copies ran while one was open for 3% of the time, Pallas kernels for 0%

commit v1 on v0

v1 whole, which is shorter than its diff:
```python
import jax
import jax.numpy as jnp
from jax import lax
from jax.sharding import PartitionSpec as P


HEADROOM = 14.0
TAG_ROWS = 16
SMALLEST = 2.0**-100


def power_of_two(n):
    return n & (n - 1) == 0


def fallback(src_fields, det_fields, probes):
    src_count, vox_count = src_fields.shape
    groups = lax.axis_size("blk")
    weighted = (src_fields.astype(jnp.float32)[None] * probes.astype(jnp.float32)[:, None]).astype(jnp.bfloat16)
    weighted = weighted.reshape(-1, vox_count)
    det_all = lax.all_gather(det_fields, "blk", axis=0, tiled=True)
    product = jnp.einsum("rv,dv->rd", weighted, det_all, preferred_element_type=jnp.float32)
    measured_b = lax.psum(product, "vox").astype(jnp.bfloat16)
    backproj = jnp.dot(measured_b, det_all, preferred_element_type=jnp.float32)
    backproj = backproj.reshape(-1, src_count, vox_count)
    contrib = jnp.sum(src_fields.astype(jnp.float32)[None] * backproj, axis=1)
    normalizer = jnp.float32(1.0 / (src_count * groups * det_all.shape[0]))
    return lax.psum(contrib, "blk") * normalizer


def pack(values, exponent):
    scaled = (values * jnp.exp2(HEADROOM - exponent)).astype(jnp.float16)
    tag = jnp.broadcast_to(exponent.astype(jnp.float16), (TAG_ROWS, values.shape[1]))
    return jnp.concatenate([scaled, tag], axis=0)


def unpack(packed):
    exponent = packed[-TAG_ROWS:][:1].astype(jnp.float32)
    return packed[:-TAG_ROWS].astype(jnp.float32) * jnp.exp2(exponent - HEADROOM), exponent


def product(src_fields, det_fields, probes):
    src_count, vox_count = src_fields.shape
    det_count = det_fields.shape[0]
    probe_count = probes.shape[0]
    groups = lax.axis_size("blk")
    slabs = lax.axis_size("vox")
    if groups < 4 or not power_of_two(groups) or not power_of_two(slabs):
        return fallback(src_fields, det_fields, probes)

    def exchange(array, chip_mask, slab_mask, cross):
        pairs = []
        for b in range(groups):
            for u in range(slabs):
                core = cross if cross < 2 else u.bit_count() & 1
                pairs.append((b * slabs + u, (b ^ (2 * chip_mask) ^ core) * slabs + (u ^ slab_mask)))
        return lax.ppermute(array, ("blk", "vox"), pairs)

    others = [exchange(det_fields, m, 0, 2) for m in range(1, groups // 2)]
    partner = exchange(src_fields, 0, 0, 1)
    probe_rows = probes.astype(jnp.float32)[:, None]

    def weigh(src):
        return (src.astype(jnp.float32)[None] * probe_rows).astype(jnp.bfloat16).reshape(-1, vox_count)

    weighted = jnp.concatenate([weigh(src_fields), weigh(partner)], axis=0)
    src = jnp.concatenate([src_fields, partner], axis=0)

    def measure(det):
        return jnp.einsum("dv,rv->dr", det, weighted, preferred_element_type=jnp.float32)

    odd = lax.population_count(lax.axis_index("vox")) & 1

    def own_order(columns):
        half = columns.shape[1] // 2
        return jnp.where(odd == 1, jnp.concatenate([columns[:, half:], columns[:, :half]], axis=1), columns)

    def total_over_slabs(measured, cross):
        exponent = jnp.ceil(jnp.log2(jnp.maximum(jnp.max(jnp.abs(measured), axis=0, keepdims=True), SMALLEST)))
        width = 1
        while width < slabs:
            sent = exchange(pack(measured, exponent), 0, width, cross)
            received, other = unpack(sent)
            measured = measured + received
            exponent = jnp.maximum(exponent, other) + 1.0
            width *= 2
        return measured.astype(jnp.bfloat16)

    def project(measured_b, det):
        rows = measured_b.reshape(-1, 2, probe_count, src_count).transpose(2, 0, 1, 3).reshape(-1, 2 * src_count)
        back = jnp.dot(rows, src, preferred_element_type=jnp.float32)
        back = back.reshape(probe_count, -1, vox_count)
        return jnp.sum(det.astype(jnp.float32)[None] * back, axis=1)

    near = total_over_slabs(measure(det_fields), 0)
    total = project(near, det_fields)
    far_det = others[0] if len(others) == 1 else jnp.concatenate(others, axis=0)
    measured = own_order(measure(far_det))
    far = own_order(total_over_slabs(measured, 1))
    total = total + project(far, far_det)
    cross, mask = 1, 1
    while mask < groups // 2:
        total = total + exchange(total, mask, 0, cross)
        cross, mask = 0, 2 * mask
    total = total + exchange(total, 0, 0, 1)
    return total * jnp.float32(1.0 / (src_count * groups * det_count * groups))


def solution(mesh):
    return jax.shard_map(
        product,
        mesh=mesh,
        in_specs=(P("blk", "vox"), P("blk", "vox"), P(None, "vox")),
        out_specs=P(None, "vox"),
        check_vma=False,
    )
```

time: 94.1 us -> 39.9 us (0.42)
  blocking collectives: 48.8 us -> 0 us
  between operations: 13.4 us -> 0.31 us
  starting transfers between devices: 0.01 us -> 12.5 us
  waiting for transfers between devices: 24.7 us -> 18.2 us
  local copies, waits for them, and re-layouts: 0.01 us -> 1.16 us
    psum x2 -> x0, blocking collectives: 48.8 us -> none  [the longest x1 38.3 us: shards(): measured = lax.psum(partial_value, 'vox')]
    all_gather x1 -> x0, waiting for transfers between devices: 24 us -> none  [shards(): lax.all_gather(det_fields, 'blk', axis=0, tiled=True)]
    ppermute x0 -> x10, waiting for transfers between devices: none -> 18.2 us  [exchange(): return lax.ppermute(array, ('blk', 'vox'), pairs)]
    ppermute x0 -> x10, starting transfers between devices: none -> 12.5 us  [exchange(): return lax.ppermute(array, ('blk', 'vox'), pairs)]
    dot_general x2 -> x4, matrix products: 3.39 us -> 3.47 us  [the longest x2 2.58 us: measure(): jnp.einsum('dv,rv->dr', det, weighted, preferred_element_type=jnp.float32)]
    convert_element_type x3 -> x18, other arithmetic: 2.99 us -> 2.99 us  [the longest x2 1.18 us: weigh(): src.astype(jnp.float32)[None] * probe_rows]
  transfers between devices with their start and end apart: 1 -> 10, of which waited for: 1 -> 7; matrix products, arithmetic and copies ran while one was open for 3% -> 11% of each run, Pallas kernels for 0% -> 0%
where the time goes in v1:
time: 39.9 us; the launch traced here: 39.6 us
  waiting for transfers between devices  18.2 us (46%)
  starting transfers between devices  12.5 us (31%)
  other arithmetic  3.89 us (10%)
  matrix products  3.47 us (9%)
  local copies, waits for them, and re-layouts  1.16 us (3%)
    ppermute x10, waiting for transfers between devices, exchange(): return lax.ppermute(array, ('blk', 'vox'), pairs)  18.2 us
    ppermute x10, starting transfers between devices, exchange(): return lax.ppermute(array, ('blk', 'vox'), pairs)  12.5 us
    dot_general x2, matrix products, measure(): jnp.einsum('dv,rv->dr', det, weighted, preferred_element_type=jnp.float32)  2.58 us
    convert_element_type x2, other arithmetic, weigh(): src.astype(jnp.float32)[None] * probe_rows  1.18 us
    convert_element_type x2, other arithmetic, project(): return jnp.sum(det.astype(jnp.float32)[None] * back, axis=1)  1.18 us
    dot_general x2, matrix products, project(): back = jnp.dot(rows, src, preferred_element_type=jnp.float32)  0.9 us
  transfers between devices with their start and end apart: 10, of which 7 were waited for; matrix products, arithmetic and copies ran while one was open for 11% of the time, Pallas kernels for 0%

profile of v1, /device:TPU:0, one launch (start us, length us, event | category | flops | bytes accessed | tf_op | source)
XLA Modules:
  0.0 39.6 jit_solution(12332506075763320094)
XLA Ops:
  0.0 0.5 %collective-permute-start = (bf16[64,4096]{1,0:T(8,128)(2,1)}, bf16[64,4096]{1,0:T(8,128)(2,1)S(1)}, u32[]{:S(2)}, u32[]{:S(2)}) collective-permute-start(bf16[64,4096]{1,0:T(8,128)(2,1)} %param.3), channel_id=1, source_target_pairs={{0,8},{1,9},{2,10},{3,11},{4,12},{5,13},{6,14},{7,15},{8,0},{9,1},... | collective-permute-start | bytes 1572872 | tf_op jit(solution)/shard_map/ppermute | solution.py:57
  0.5 2.5 %collective-permute-start.4 = (bf16[64,4096]{1,0:T(8,128)(2,1)}, bf16[64,4096]{1,0:T(8,128)(2,1)}, u32[]{:S(2)}, u32[]{:S(2)}) collective-permute-start(bf16[64,4096]{1,0:T(8,128)(2,1)} %param.4), channel_id=1, source_target_pairs={{0,16},{1,25},{2,26},{3,19},{4,28},{5,21},{6,22},{7,31},{8,24},{9,... | collective-permute-start | bytes 1572872 | tf_op jit(solution)/shard_map/ppermute | solution.py:57
  3.0 1.1 %convert_element_type.118 = f32[64,4096]{1,0:T(8,128)S(1)} convert(bf16[64,4096]{1,0:T(8,128)(2,1)} %param.3) | non-fusion elementwise | flops 262144 | bytes 1572864 | tf_op jit(solution)/shard_map/convert_element_type | solution.py:64
  4.2 0.1 convert_element_type.117
  4.3 0.6 %copy-done.2 = bf16[2,4096]{1,0:T(2,128)(2,1)S(1)} copy-done((bf16[2,4096]{1,0:T(2,128)(2,1)S(1)}, bf16[2,4096]{1,0:T(2,128)(2,1)}, u32[]{:S(2)}) %copy-start.2) | copy-done | bytes 16408
  4.9 0.1 convert_element_type.122
  5.0 0.4 multiply_convert_fusion.1
  5.3 0.8 %abs_reduce_fusion.1 = (f32[256]{0:T(256)S(1)}, f32[64,256]{1,0:T(8,128)S(1)}) fusion(bf16[64,4096]{1,0:T(8,128)(2,1)S(1)} %copy-done, bf16[128,4096]{1,0:T(8,128)(2,1)S(1)} %bitcast.32, bf16[128,4096]{1,0:T(8,128)(2,1)S(1)} %bitcast.30), kind=kOutput, calls=%fused_computation.26 | convolution fusion | flops 138444544 | bytes 2688000 | tf_op jit(solution)/shard_map/dv,rv->dr/dot_general | solution.py:70
  6.1 9.8 %collective-permute-done.4 = bf16[64,4096]{1,0:T(8,128)(2,1)} collective-permute-done((bf16[64,4096]{1,0:T(8,128)(2,1)}, bf16[64,4096]{1,0:T(8,128)(2,1)}, u32[]{:S(2)}, u32[]{:S(2)}) %collective-permute-start.4) | collective-permute-done | bytes 524320 | tf_op jit(solution)/shard_map/ppermute | solution.py:57
  15.9 1.8 %fusion.4 = f32[64,256]{1,0:T(8,128)S(1)} fusion(bf16[64,4096]{1,0:T(8,128)(2,1)} %collective-permute-done.4, bf16[128,4096]{1,0:T(8,128)(2,1)S(1)} %bitcast.33, bf16[128,4096]{1,0:T(8,128)(2,1)S(1)} %bitcast.31), kind=kOutput, calls=%fused_computation.9 | convolution fusion | flops 138412032 | bytes 2686976 | tf_op jit(solution)/shard_map/dv,rv->dr/dot_general | solution.py:70
  17.8 1.2 %collective-permute-start.5 = (f16[80,256]{1,0:T(8,128)(2,1)S(1)}, f16[80,256]{1,0:T(8,128)(2,1)S(1)}, u32[]{:S(2)}, u32[]{:S(2)}) collective-permute-start(f16[80,256]{1,0:T(8,128)(2,1)S(1)} %pad_maximum_fusion.10), channel_id=1, source_target_pairs={{0,9},{1,8},{2,11},{3,10},{4,13},{5,12},{6,15},{7,14},{8,1},{9,0},... | collective-permute-start | bytes 122888 | tf_op jit(solution)/shard_map/ppermute | solution.py:57
  19.1 0.4 %collective-permute-start.1 = (f16[80,256]{1,0:T(8,128)(2,1)S(1)}, f16[80,256]{1,0:T(8,128)(2,1)S(1)}, u32[]{:S(2)}, u32[]{:S(2)}) collective-permute-start(f16[80,256]{1,0:T(8,128)(2,1)S(1)} %pad_maximum_fusion.7), channel_id=1, source_target_pairs={{0,1},{1,0},{2,3},{3,2},{4,5},{5,4},{6,7},{7,6},{8,9},{9,8},{10,11... | collective-permute-start | bytes 122888 | tf_op jit(solution)/shard_map/ppermute | solution.py:57
  19.5 1.1 %convert_element_type.138 = f32[64,4096]{1,0:T(8,128)S(1)} convert(bf16[64,4096]{1,0:T(8,128)(2,1)} %collective-permute-done.4) | non-fusion elementwise | flops 262144 | bytes 1572864 | tf_op jit(solution)/shard_map/convert_element_type | solution.py:93
  20.6 1.1 %collective-permute-done.5 = f16[80,256]{1,0:T(8,128)(2,1)S(1)} collective-permute-done((f16[80,256]{1,0:T(8,128)(2,1)S(1)}, f16[80,256]{1,0:T(8,128)(2,1)S(1)}, u32[]{:S(2)}, u32[]{:S(2)}) %collective-permute-start.5) | collective-permute-done | bytes 40992 | tf_op jit(solution)/shard_map/ppermute | solution.py:57
  21.8 1.0 %collective-permute-start.6 = (f16[80,256]{1,0:T(8,128)(2,1)S(1)}, f16[80,256]{1,0:T(8,128)(2,1)S(1)}, u32[]{:S(2)}, u32[]{:S(2)}) collective-permute-start(f16[80,256]{1,0:T(8,128)(2,1)S(1)} %pad_maximum_fusion.11), channel_id=1, source_target_pairs={{0,10},{1,11},{2,8},{3,9},{4,14},{5,15},{6,12},{7,13},{8,2},{9,3},... | collective-permute-start | bytes 122888 | tf_op jit(solution)/shard_map/ppermute | solution.py:57
  22.8 0.4 collective-permute-done.1
  23.2 1.9 %collective-permute-start.2 = (f16[80,256]{1,0:T(8,128)(2,1)S(1)}, f16[80,256]{1,0:T(8,128)(2,1)S(1)}, u32[]{:S(2)}, u32[]{:S(2)}) collective-permute-start(f16[80,256]{1,0:T(8,128)(2,1)S(1)} %pad_maximum_fusion.8), channel_id=1, source_target_pairs={{0,2},{1,3},{2,0},{3,1},{4,6},{5,7},{6,4},{7,5},{8,10},{9,11},{10,... | collective-permute-start | bytes 122888 | tf_op jit(solution)/shard_map/ppermute | solution.py:57
  25.1 0.3 collective-permute-done.6
  25.5 2.1 %collective-permute-start.7 = (f16[80,256]{1,0:T(8,128)(2,1)S(1)}, f16[80,256]{1,0:T(8,128)(2,1)S(1)}, u32[]{:S(2)}, u32[]{:S(2)}) collective-permute-start(f16[80,256]{1,0:T(8,128)(2,1)S(1)} %pad_maximum_fusion.12), channel_id=1, source_target_pairs={{0,12},{1,13},{2,14},{3,15},{4,8},{5,9},{6,10},{7,11},{8,4},{9,5},... | collective-permute-start | bytes 122888 | tf_op jit(solution)/shard_map/ppermute | solution.py:57
  27.8 2.5 %collective-permute-start.3 = (f16[80,256]{1,0:T(8,128)(2,1)S(1)}, f16[80,256]{1,0:T(8,128)(2,1)S(1)}, u32[]{:S(2)}, u32[]{:S(2)}) collective-permute-start(f16[80,256]{1,0:T(8,128)(2,1)S(1)} %pad_maximum_fusion.9), channel_id=1, source_target_pairs={{0,4},{1,5},{2,6},{3,7},{4,0},{5,1},{6,2},{7,3},{8,12},{9,13},{10,... | collective-permute-start | bytes 122888 | tf_op jit(solution)/shard_map/ppermute | solution.py:57
  30.4 0.1 reshape.106
  30.5 0.1 dot_general.26
  30.6 2.1 %collective-permute-done.3 = f16[80,256]{1,0:T(8,128)(2,1)S(1)} collective-permute-done((f16[80,256]{1,0:T(8,128)(2,1)S(1)}, f16[80,256]{1,0:T(8,128)(2,1)S(1)}, u32[]{:S(2)}, u32[]{:S(2)}) %collective-permute-start.3) | collective-permute-done | bytes 40992 | tf_op jit(solution)/shard_map/ppermute | solution.py:57
  32.8 0.1 reshape.105
  32.9 0.1 dot_general.22
  33.0 0.5 %multiply_reduce_fusion = f32[2,4096]{1,0:T(2,128)S(1)} fusion(f32[64,4096]{1,0:T(8,128)S(1)} %convert_element_type.138, bf16[2,64,128]{2,1,0:T(8,128)(2,1)S(1)} %dot_general.26, bf16[64,4096]{1,0:T(8,128)(2,1)S(1)} %collective-permute-done, bf16[64,4096]{1,0:T(8,128)(2,1)S(1)} %copy-done.1), kind=kOutput, calls=%fused_computation.2 | convolution fusion | flops 137355264 | bytes 2162688 | tf_op jit(solution)/shard_map/dot_general | solution.py:91
  33.5 0.4 %fusion = f32[2,4096]{1,0:T(2,128)S(1)} fusion(bf16[2,64,128]{2,1,0:T(8,128)(2,1)S(1)} %dot_general.22, f32[64,4096]{1,0:T(8,128)S(1)} %convert_element_type.117, bf16[64,4096]{1,0:T(8,128)(2,1)S(1)} %collective-permute-done, bf16[64,4096]{1,0:T(8,128)(2,1)S(1)} %copy-done.1), kind=kOutput, calls=%fused_computation.5 | convolution fusion | flops 137355264 | bytes 2162688 | tf_op jit(solution)/shard_map/dot_general | solution.py:91
  34.0 0.2 collective-permute-start.8
  34.2 3.5 %collective-permute-done.8 = f32[2,4096]{1,0:T(2,128)S(1)} collective-permute-done((f32[2,4096]{1,0:T(2,128)S(1)}, f32[2,4096]{1,0:T(2,128)S(1)}, u32[]{:S(2)}, u32[]{:S(2)}) %collective-permute-start.8) | collective-permute-done | bytes 32800 | tf_op jit(solution)/shard_map/ppermute | solution.py:57
  37.7 0.2 collective-permute-start.9
  37.9 1.1 %collective-permute-done.9 = f32[2,4096]{1,0:T(2,128)S(1)} collective-permute-done((f32[2,4096]{1,0:T(2,128)S(1)}, f32[2,4096]{1,0:T(2,128)S(1)}, u32[]{:S(2)}, u32[]{:S(2)}) %collective-permute-start.9) | collective-permute-done | bytes 32800 | tf_op jit(solution)/shard_map/ppermute | solution.py:57
  39.0 0.6 %add_multiply_fusion = f32[2,4096]{1,0:T(2,128)} fusion(f32[2,4096]{1,0:T(2,128)S(1)} %add.56, f32[2,4096]{1,0:T(2,128)S(1)} %collective-permute-done.9), kind=kLoop, calls=%fused_computation.34 | loop fusion | flops 16384 | bytes 98304 | tf_op jit(solution)/shard_map/mul | solution.py:106
  (49 shorter events, 0.7 us)
Async XLA Ops:
  0.0 4.2 %copy-start = (bf16[64,4096]{1,0:T(8,128)(2,1)S(1)}, bf16[64,4096]{1,0:T(8,128)(2,1)}, u32[]{:S(2)}) copy-start(bf16[64,4096]{1,0:T(8,128)(2,1)} %param.4) | copy-start | bytes 1572868
  0.0 4.9 %collective-permute-start = (bf16[64,4096]{1,0:T(8,128)(2,1)}, bf16[64,4096]{1,0:T(8,128)(2,1)S(1)}, u32[]{:S(2)}, u32[]{:S(2)}) collective-permute-start(bf16[64,4096]{1,0:T(8,128)(2,1)} %param.3), channel_id=1, source_target_pairs={{0,8},{1,9},{2,10},{3,11},{4,12},{5,13},{6,14},{7,15},{8,0},{9,1},... | collective-permute-start | bytes 1572872 | tf_op jit(solution)/shard_map/ppermute | solution.py:57
  0.5 15.4 %collective-permute-start.4 = (bf16[64,4096]{1,0:T(8,128)(2,1)}, bf16[64,4096]{1,0:T(8,128)(2,1)}, u32[]{:S(2)}, u32[]{:S(2)}) collective-permute-start(bf16[64,4096]{1,0:T(8,128)(2,1)} %param.4), channel_id=1, source_target_pairs={{0,16},{1,25},{2,26},{3,19},{4,28},{5,21},{6,22},{7,31},{8,24},{9,... | collective-permute-start | bytes 1572872 | tf_op jit(solution)/shard_map/ppermute | solution.py:57
  4.1 0.7 %copy-start.2 = (bf16[2,4096]{1,0:T(2,128)(2,1)S(1)}, bf16[2,4096]{1,0:T(2,128)(2,1)}, u32[]{:S(2)}) copy-start(bf16[2,4096]{1,0:T(2,128)(2,1)} %param.5) | copy-start | bytes 49156
  17.8 3.9 %collective-permute-start.5 = (f16[80,256]{1,0:T(8,128)(2,1)S(1)}, f16[80,256]{1,0:T(8,128)(2,1)S(1)}, u32[]{:S(2)}, u32[]{:S(2)}) collective-permute-start(f16[80,256]{1,0:T(8,128)(2,1)S(1)} %pad_maximum_fusion.10), channel_id=1, source_target_pairs={{0,9},{1,8},{2,11},{3,10},{4,13},{5,12},{6,15},{7,14},{8,1},{9,0},... | collective-permute-start | bytes 122888 | tf_op jit(solution)/shard_map/ppermute | solution.py:57
  19.1 4.1 %collective-permute-start.1 = (f16[80,256]{1,0:T(8,128)(2,1)S(1)}, f16[80,256]{1,0:T(8,128)(2,1)S(1)}, u32[]{:S(2)}, u32[]{:S(2)}) collective-permute-start(f16[80,256]{1,0:T(8,128)(2,1)S(1)} %pad_maximum_fusion.7), channel_id=1, source_target_pairs={{0,1},{1,0},{2,3},{3,2},{4,5},{5,4},{6,7},{7,6},{8,9},{9,8},{10,11... | collective-permute-start | bytes 122888 | tf_op jit(solution)/shard_map/ppermute | solution.py:57
  21.8 11.3 %copy-start.1 = (bf16[64,4096]{1,0:T(8,128)(2,1)S(1)}, bf16[64,4096]{1,0:T(8,128)(2,1)}, u32[]{:S(2)}) copy-start(bf16[64,4096]{1,0:T(8,128)(2,1)} %param.3) | copy-start | bytes 1572868
  21.8 3.6 %collective-permute-start.6 = (f16[80,256]{1,0:T(8,128)(2,1)S(1)}, f16[80,256]{1,0:T(8,128)(2,1)S(1)}, u32[]{:S(2)}, u32[]{:S(2)}) collective-permute-start(f16[80,256]{1,0:T(8,128)(2,1)S(1)} %pad_maximum_fusion.11), channel_id=1, source_target_pairs={{0,10},{1,11},{2,8},{3,9},{4,14},{5,15},{6,12},{7,13},{8,2},{9,3},... | collective-permute-start | bytes 122888 | tf_op jit(solution)/shard_map/ppermute | solution.py:57
  23.2 4.4 %collective-permute-start.2 = (f16[80,256]{1,0:T(8,128)(2,1)S(1)}, f16[80,256]{1,0:T(8,128)(2,1)S(1)}, u32[]{:S(2)}, u32[]{:S(2)}) collective-permute-start(f16[80,256]{1,0:T(8,128)(2,1)S(1)} %pad_maximum_fusion.8), channel_id=1, source_target_pairs={{0,2},{1,3},{2,0},{3,1},{4,6},{5,7},{6,4},{7,5},{8,10},{9,11},{10,... | collective-permute-start | bytes 122888 | tf_op jit(solution)/shard_map/ppermute | solution.py:57
  25.5 4.7 %collective-permute-start.7 = (f16[80,256]{1,0:T(8,128)(2,1)S(1)}, f16[80,256]{1,0:T(8,128)(2,1)S(1)}, u32[]{:S(2)}, u32[]{:S(2)}) collective-permute-start(f16[80,256]{1,0:T(8,128)(2,1)S(1)} %pad_maximum_fusion.12), channel_id=1, source_target_pairs={{0,12},{1,13},{2,14},{3,15},{4,8},{5,9},{6,10},{7,11},{8,4},{9,5},... | collective-permute-start | bytes 122888 | tf_op jit(solution)/shard_map/ppermute | solution.py:57
  27.8 5.0 %collective-permute-start.3 = (f16[80,256]{1,0:T(8,128)(2,1)S(1)}, f16[80,256]{1,0:T(8,128)(2,1)S(1)}, u32[]{:S(2)}, u32[]{:S(2)}) collective-permute-start(f16[80,256]{1,0:T(8,128)(2,1)S(1)} %pad_maximum_fusion.9), channel_id=1, source_target_pairs={{0,4},{1,5},{2,6},{3,7},{4,0},{5,1},{6,2},{7,3},{8,12},{9,13},{10,... | collective-permute-start | bytes 122888 | tf_op jit(solution)/shard_map/ppermute | solution.py:57
  34.0 3.7 %collective-permute-start.8 = (f32[2,4096]{1,0:T(2,128)S(1)}, f32[2,4096]{1,0:T(2,128)S(1)}, u32[]{:S(2)}, u32[]{:S(2)}) collective-permute-start(f32[2,4096]{1,0:T(2,128)S(1)} %add.55), channel_id=1, source_target_pairs={{0,24},{1,25},{2,26},{3,27},{4,28},{5,29},{6,30},{7,31},{8,16},{9,... | collective-permute-start | bytes 98312 | tf_op jit(solution)/shard_map/ppermute | solution.py:57
  37.7 1.3 %collective-permute-start.9 = (f32[2,4096]{1,0:T(2,128)S(1)}, f32[2,4096]{1,0:T(2,128)S(1)}, u32[]{:S(2)}, u32[]{:S(2)}) collective-permute-start(f32[2,4096]{1,0:T(2,128)S(1)} %add.56), channel_id=1, source_target_pairs={{0,8},{1,9},{2,10},{3,11},{4,12},{5,13},{6,14},{7,15},{8,0},{9,1},... | collective-permute-start | bytes 98312 | tf_op jit(solution)/shard_map/ppermute | solution.py:57

commit v2 on v1

--- a/solution.py
+++ b/solution.py
@@ -63,17 +63,12 @@
     def weigh(src):
         return (src.astype(jnp.float32)[None] * probe_rows).astype(jnp.bfloat16).reshape(-1, vox_count)
 
-    weighted = jnp.concatenate([weigh(src_fields), weigh(partner)], axis=0)
-    src = jnp.concatenate([src_fields, partner], axis=0)
+    first = (lax.axis_index("blk") & 1) == 0
+    src = jnp.concatenate([jnp.where(first, src_fields, partner), jnp.where(first, partner, src_fields)], axis=0)
+    weighted = weigh(src)
 
     def measure(det):
         return jnp.einsum("dv,rv->dr", det, weighted, preferred_element_type=jnp.float32)
-
-    odd = lax.population_count(lax.axis_index("vox")) & 1
-
-    def own_order(columns):
-        half = columns.shape[1] // 2
-        return jnp.where(odd == 1, jnp.concatenate([columns[:, half:], columns[:, :half]], axis=1), columns)
 
     def total_over_slabs(measured, cross):
         exponent = jnp.ceil(jnp.log2(jnp.maximum(jnp.max(jnp.abs(measured), axis=0, keepdims=True), SMALLEST)))
@@ -87,7 +82,7 @@
         return measured.astype(jnp.bfloat16)
 
     def project(measured_b, det):
-        rows = measured_b.reshape(-1, 2, probe_count, src_count).transpose(2, 0, 1, 3).reshape(-1, 2 * src_count)
+        rows = measured_b.reshape(-1, probe_count, 2 * src_count).transpose(1, 0, 2).reshape(-1, 2 * src_count)
         back = jnp.dot(rows, src, preferred_element_type=jnp.float32)
         back = back.reshape(probe_count, -1, vox_count)
         return jnp.sum(det.astype(jnp.float32)[None] * back, axis=1)
@@ -95,8 +90,8 @@
     near = total_over_slabs(measure(det_fields), 0)
     total = project(near, det_fields)
     far_det = others[0] if len(others) == 1 else jnp.concatenate(others, axis=0)
-    measured = own_order(measure(far_det))
-    far = own_order(total_over_slabs(measured, 1))
+    measured = measure(far_det)
+    far = total_over_slabs(measured, 1)
     total = total + project(far, far_det)
     cross, mask = 1, 1
     while mask < groups // 2:

time: 39.9 us -> 38.5 us (0.965)
  matrix products: 3.47 us -> 2.49 us
  waiting for transfers between devices: 18.2 us -> 17.4 us
  other arithmetic: 3.89 us -> 4.66 us
  local copies, waits for them, and re-layouts: 1.16 us -> 0.73 us
    select_n x1, other arithmetic: 0.02 us -> 1.12 us  [product(): jnp.where(first, src_fields, partner)]
    dot_general x2, matrix products: 2.58 us -> 1.55 us  [measure(): jnp.einsum('dv,rv->dr', det, weighted, preferred_element_type=jnp.float32)]
    convert_element_type x2 -> x1, other arithmetic: 1.18 us -> 0.21 us  [weigh(): src.astype(jnp.float32)[None] * probe_rows]
    ppermute x10, waiting for transfers between devices: 18.2 us -> 17.4 us  [exchange(): return lax.ppermute(array, ('blk', 'vox'), pairs)]
    convert_element_type x1, other arithmetic: 0.01 us -> 0.73 us  [product(): probe_rows = probes.astype(jnp.float32)[:, None]]
  transfers between devices with their start and end apart: 10 -> 10, of which waited for: 7 -> 7; matrix products, arithmetic and copies ran while one was open for 11% -> 12% of each run, Pallas kernels for 0% -> 0%
where the time goes in v2:
time: 38.5 us; the launch traced here: 38.2 us
  waiting for transfers between devices  17.4 us (45%)
  starting transfers between devices  12.8 us (33%)
  other arithmetic  4.66 us (12%)
  matrix products  2.49 us (6%)
  local copies, waits for them, and re-layouts  0.73 us (2%)
    ppermute x10, waiting for transfers between devices, exchange(): return lax.ppermute(array, ('blk', 'vox'), pairs)  17.4 us
    ppermute x10, starting transfers between devices, exchange(): return lax.ppermute(array, ('blk', 'vox'), pairs)  12.8 us
    dot_general x2, matrix products, measure(): jnp.einsum('dv,rv->dr', det, weighted, preferred_element_type=jnp.float32)  1.55 us
    convert_element_type x2, other arithmetic, project(): return jnp.sum(det.astype(jnp.float32)[None] * back, axis=1)  1.21 us
    select_n x1, other arithmetic, product(): jnp.where(first, src_fields, partner)  1.12 us
    dot_general x2, matrix products, project(): back = jnp.dot(rows, src, preferred_element_type=jnp.float32)  0.94 us
  transfers between devices with their start and end apart: 10, of which 7 were waited for; matrix products, arithmetic and copies ran while one was open for 12% of the time, Pallas kernels for 0%

profile of v2, /device:TPU:0, one launch (start us, length us, event | category | flops | bytes accessed | tf_op | source)
XLA Modules:
  0.0 38.2 jit_solution(8953192101639789967)
XLA Ops:
  0.0 0.5 %collective-permute-start = (bf16[64,4096]{1,0:T(8,128)(2,1)}, bf16[64,4096]{1,0:T(8,128)(2,1)S(1)}, u32[]{:S(2)}, u32[]{:S(2)}) collective-permute-start(bf16[64,4096]{1,0:T(8,128)(2,1)} %param.3), channel_id=1, source_target_pairs={{0,8},{1,9},{2,10},{3,11},{4,12},{5,13},{6,14},{7,15},{8,0},{9,1},... | collective-permute-start | bytes 1572872 | tf_op jit(solution)/shard_map/ppermute | solution.py:57
  0.5 2.5 %collective-permute-start.4 = (bf16[64,4096]{1,0:T(8,128)(2,1)}, bf16[64,4096]{1,0:T(8,128)(2,1)S(1)}, u32[]{:S(2)}, u32[]{:S(2)}) collective-permute-start(bf16[64,4096]{1,0:T(8,128)(2,1)} %param.4), channel_id=1, source_target_pairs={{0,16},{1,25},{2,26},{3,19},{4,28},{5,21},{6,22},{7,31},{8,24},{9,... | collective-permute-start | bytes 1572872 | tf_op jit(solution)/shard_map/ppermute | solution.py:57
  3.0 1.1 %convert_element_type.111 = f32[64,4096]{1,0:T(8,128)S(1)} convert(bf16[64,4096]{1,0:T(8,128)(2,1)} %param.4) | non-fusion elementwise | flops 262144 | bytes 1572864 | tf_op jit(solution)/shard_map/convert_element_type | solution.py:88
  4.1 0.7 %convert_element_type.113 = f32[2,4096]{1,0:T(2,128)S(1)} convert(bf16[2,4096]{1,0:T(2,128)(2,1)} %param.5) | non-fusion elementwise | flops 8192 | bytes 49152 | tf_op jit(solution)/shard_map/convert_element_type | solution.py:61
  4.9 0.0 collective-permute-done
  4.9 1.1 %broadcast_select_fusion.1 = (bf16[64,4096]{1,0:T(8,128)(2,1)S(1)}, bf16[64,4096]{1,0:T(8,128)(2,1)S(1)}) fusion(bf16[64,4096]{1,0:T(8,128)(2,1)} %param.3, bf16[64,4096]{1,0:T(8,128)(2,1)S(1)} %collective-permute-done, pred[]{:T(512)S(6)} %eq.3), kind=kLoop, calls=%fused_computation.11 | loop fusion | flops 524288 | bytes 2097153 | tf_op jit(solution)/shard_map/jit(_where)/select_n | solution.py:67
  6.0 0.2 fusion.4
  6.2 0.0 copy-start
  6.2 0.3 multiply_convert_fusion
  6.6 0.7 %copy-done = bf16[64,4096]{1,0:T(8,128)(2,1)S(1)} copy-done((bf16[64,4096]{1,0:T(8,128)(2,1)S(1)}, bf16[64,4096]{1,0:T(8,128)(2,1)}, u32[]{:S(2)}) %copy-start) | copy-done | bytes 524312
  7.3 0.8 %abs_reduce_fusion.1 = (f32[256]{0:T(256)S(1)}, f32[64,256]{1,0:T(8,128)S(1)}) fusion(bf16[256,4096]{1,0:T(8,128)(2,1)S(1)} %bitcast.48, bf16[64,4096]{1,0:T(8,128)(2,1)S(1)} %copy-done), kind=kOutput, calls=%fused_computation.26 | convolution fusion | flops 134250240 | bytes 2688000 | tf_op jit(solution)/shard_map/dv,rv->dr/dot_general | solution.py:71
  8.0 7.7 %collective-permute-done.4 = bf16[64,4096]{1,0:T(8,128)(2,1)S(1)} collective-permute-done((bf16[64,4096]{1,0:T(8,128)(2,1)}, bf16[64,4096]{1,0:T(8,128)(2,1)S(1)}, u32[]{:S(2)}, u32[]{:S(2)}) %collective-permute-start.4) | collective-permute-done | bytes 524320 | tf_op jit(solution)/shard_map/ppermute | solution.py:57
  15.8 0.8 %abs_reduce_fusion = (f32[256]{0:T(256)S(1)}, f32[64,256]{1,0:T(8,128)S(1)}) fusion(bf16[256,4096]{1,0:T(8,128)(2,1)S(1)} %bitcast.49, bf16[64,4096]{1,0:T(8,128)(2,1)S(1)} %collective-permute-done.4), kind=kOutput, calls=%fused_computation.19 | convolution fusion | flops 134250240 | bytes 2688000 | tf_op jit(solution)/shard_map/dv,rv->dr/dot_general | solution.py:71
  16.6 1.1 %collective-permute-start.5 = (f16[80,256]{1,0:T(8,128)(2,1)S(1)}, f16[80,256]{1,0:T(8,128)(2,1)S(1)}, u32[]{:S(2)}, u32[]{:S(2)}) collective-permute-start(f16[80,256]{1,0:T(8,128)(2,1)S(1)} %pad_maximum_fusion.6), channel_id=1, source_target_pairs={{0,9},{1,8},{2,11},{3,10},{4,13},{5,12},{6,15},{7,14},{8,1},{9,0},... | collective-permute-start | bytes 122888 | tf_op jit(solution)/shard_map/ppermute | solution.py:57
  17.9 0.5 %collective-permute-start.1 = (f16[80,256]{1,0:T(8,128)(2,1)S(1)}, f16[80,256]{1,0:T(8,128)(2,1)S(1)}, u32[]{:S(2)}, u32[]{:S(2)}) collective-permute-start(f16[80,256]{1,0:T(8,128)(2,1)S(1)} %pad_maximum_fusion.3), channel_id=1, source_target_pairs={{0,1},{1,0},{2,3},{3,2},{4,5},{5,4},{6,7},{7,6},{8,9},{9,8},{10,11... | collective-permute-start | bytes 122888 | tf_op jit(solution)/shard_map/ppermute | solution.py:57
  18.4 0.1 convert_element_type.129
  18.5 2.0 %collective-permute-done.5 = f16[80,256]{1,0:T(8,128)(2,1)S(1)} collective-permute-done((f16[80,256]{1,0:T(8,128)(2,1)S(1)}, f16[80,256]{1,0:T(8,128)(2,1)S(1)}, u32[]{:S(2)}, u32[]{:S(2)}) %collective-permute-start.5) | collective-permute-done | bytes 40992 | tf_op jit(solution)/shard_map/ppermute | solution.py:57
  20.5 1.1 %collective-permute-start.6 = (f16[80,256]{1,0:T(8,128)(2,1)S(1)}, f16[80,256]{1,0:T(8,128)(2,1)S(1)}, u32[]{:S(2)}, u32[]{:S(2)}) collective-permute-start(f16[80,256]{1,0:T(8,128)(2,1)S(1)} %pad_maximum_fusion.7), channel_id=1, source_target_pairs={{0,10},{1,11},{2,8},{3,9},{4,14},{5,15},{6,12},{7,13},{8,2},{9,3},... | collective-permute-start | bytes 122888 | tf_op jit(solution)/shard_map/ppermute | solution.py:57
  21.6 0.3 collective-permute-done.1
  22.0 1.9 %collective-permute-start.2 = (f16[80,256]{1,0:T(8,128)(2,1)S(1)}, f16[80,256]{1,0:T(8,128)(2,1)S(1)}, u32[]{:S(2)}, u32[]{:S(2)}) collective-permute-start(f16[80,256]{1,0:T(8,128)(2,1)S(1)} %pad_maximum_fusion.4), channel_id=1, source_target_pairs={{0,2},{1,3},{2,0},{3,1},{4,6},{5,7},{6,4},{7,5},{8,10},{9,11},{10,... | collective-permute-start | bytes 122888 | tf_op jit(solution)/shard_map/ppermute | solution.py:57
  23.9 0.3 collective-permute-done.6
  24.3 2.3 %collective-permute-start.7 = (f16[80,256]{1,0:T(8,128)(2,1)S(1)}, f16[80,256]{1,0:T(8,128)(2,1)S(1)}, u32[]{:S(2)}, u32[]{:S(2)}) collective-permute-start(f16[80,256]{1,0:T(8,128)(2,1)S(1)} %pad_maximum_fusion.8), channel_id=1, source_target_pairs={{0,12},{1,13},{2,14},{3,15},{4,8},{5,9},{6,10},{7,11},{8,4},{9,5},... | collective-permute-start | bytes 122888 | tf_op jit(solution)/shard_map/ppermute | solution.py:57
  26.5 0.0 collective-permute-done.2
  26.6 2.5 %collective-permute-start.3 = (f16[80,256]{1,0:T(8,128)(2,1)S(1)}, f16[80,256]{1,0:T(8,128)(2,1)S(1)}, u32[]{:S(2)}, u32[]{:S(2)}) collective-permute-start(f16[80,256]{1,0:T(8,128)(2,1)S(1)} %pad_maximum_fusion.5), channel_id=1, source_target_pairs={{0,4},{1,5},{2,6},{3,7},{4,0},{5,1},{6,2},{7,3},{8,12},{9,13},{10,... | collective-permute-start | bytes 122888 | tf_op jit(solution)/shard_map/ppermute | solution.py:57
  29.1 2.5 %collective-permute-done.3 = f16[80,256]{1,0:T(8,128)(2,1)S(1)} collective-permute-done((f16[80,256]{1,0:T(8,128)(2,1)S(1)}, f16[80,256]{1,0:T(8,128)(2,1)S(1)}, u32[]{:S(2)}, u32[]{:S(2)}) %collective-permute-start.3) | collective-permute-done | bytes 40992 | tf_op jit(solution)/shard_map/ppermute | solution.py:57
  31.6 0.5 %multiply_reduce_fusion = f32[2,4096]{1,0:T(2,128)S(1)} fusion(f32[64,4096]{1,0:T(8,128)S(1)} %convert_element_type.129, bf16[64,4096]{1,0:T(8,128)(2,1)S(1)} %get-tuple-element.14, bf16[64,4096]{1,0:T(8,128)(2,1)S(1)} %get-tuple-element.13, f16[80,256]{1,0:T(8,128)(2,1)S(1)} %collective-permute-done.7, f32[256]{0:T(256)S(1)} %bitcast.67, ...), kind=kOutput, calls=%fused_computation.2 | convolution fusion | flops 137519104 | bytes 2296832 | tf_op jit(solution)/shard_map/dot_general | solution.py:86
  32.1 0.5 %fusion = f32[2,4096]{1,0:T(2,128)S(1)} fusion(f32[64,4096]{1,0:T(8,128)S(1)} %convert_element_type.111, bf16[64,4096]{1,0:T(8,128)(2,1)S(1)} %get-tuple-element.14, bf16[64,4096]{1,0:T(8,128)(2,1)S(1)} %get-tuple-element.13, f16[80,256]{1,0:T(8,128)(2,1)S(1)} %collective-permute-done.3, f32[256]{0:T(256)S(1)} %bitcast.66, f32[256]{0:T(256)S(1)} %bitcast.59, ...), kind=kOutput, calls=%fused_computation.3 | convolution fusion | flops 137519104 | bytes 2296832 | tf_op jit(solution)/shard_map/dot_general | solution.py:86
  32.6 0.2 collective-permute-start.8
  32.8 3.5 %collective-permute-done.8 = f32[2,4096]{1,0:T(2,128)S(1)} collective-permute-done((f32[2,4096]{1,0:T(2,128)S(1)}, f32[2,4096]{1,0:T(2,128)S(1)}, u32[]{:S(2)}, u32[]{:S(2)}) %collective-permute-start.8) | collective-permute-done | bytes 32800 | tf_op jit(solution)/shard_map/ppermute | solution.py:57
  36.3 0.2 collective-permute-start.9
  36.5 1.1 %collective-permute-done.9 = f32[2,4096]{1,0:T(2,128)S(1)} collective-permute-done((f32[2,4096]{1,0:T(2,128)S(1)}, f32[2,4096]{1,0:T(2,128)S(1)}, u32[]{:S(2)}, u32[]{:S(2)}) %collective-permute-start.9) | collective-permute-done | bytes 32800 | tf_op jit(solution)/shard_map/ppermute | solution.py:57
  37.6 0.6 %add_multiply_fusion = f32[2,4096]{1,0:T(2,128)} fusion(f32[2,4096]{1,0:T(2,128)S(1)} %add.56, f32[2,4096]{1,0:T(2,128)S(1)} %collective-permute-done.9), kind=kLoop, calls=%fused_computation.39 | loop fusion | flops 16384 | bytes 98304 | tf_op jit(solution)/shard_map/mul | solution.py:101
  (33 shorter events, 0.5 us)
Async XLA Ops:
  0.0 4.9 %collective-permute-start = (bf16[64,4096]{1,0:T(8,128)(2,1)}, bf16[64,4096]{1,0:T(8,128)(2,1)S(1)}, u32[]{:S(2)}, u32[]{:S(2)}) collective-permute-start(bf16[64,4096]{1,0:T(8,128)(2,1)} %param.3), channel_id=1, source_target_pairs={{0,8},{1,9},{2,10},{3,11},{4,12},{5,13},{6,14},{7,15},{8,0},{9,1},... | collective-permute-start | bytes 1572872 | tf_op jit(solution)/shard_map/ppermute | solution.py:57
  0.5 15.3 %collective-permute-start.4 = (bf16[64,4096]{1,0:T(8,128)(2,1)}, bf16[64,4096]{1,0:T(8,128)(2,1)S(1)}, u32[]{:S(2)}, u32[]{:S(2)}) collective-permute-start(bf16[64,4096]{1,0:T(8,128)(2,1)} %param.4), channel_id=1, source_target_pairs={{0,16},{1,25},{2,26},{3,19},{4,28},{5,21},{6,22},{7,31},{8,24},{9,... | collective-permute-start | bytes 1572872 | tf_op jit(solution)/shard_map/ppermute | solution.py:57
  6.2 1.0 %copy-start = (bf16[64,4096]{1,0:T(8,128)(2,1)S(1)}, bf16[64,4096]{1,0:T(8,128)(2,1)}, u32[]{:S(2)}) copy-start(bf16[64,4096]{1,0:T(8,128)(2,1)} %param.4) | copy-start | bytes 1572868
  16.6 3.8 %collective-permute-start.5 = (f16[80,256]{1,0:T(8,128)(2,1)S(1)}, f16[80,256]{1,0:T(8,128)(2,1)S(1)}, u32[]{:S(2)}, u32[]{:S(2)}) collective-permute-start(f16[80,256]{1,0:T(8,128)(2,1)S(1)} %pad_maximum_fusion.6), channel_id=1, source_target_pairs={{0,9},{1,8},{2,11},{3,10},{4,13},{5,12},{6,15},{7,14},{8,1},{9,0},... | collective-permute-start | bytes 122888 | tf_op jit(solution)/shard_map/ppermute | solution.py:57
  17.9 4.1 %collective-permute-start.1 = (f16[80,256]{1,0:T(8,128)(2,1)S(1)}, f16[80,256]{1,0:T(8,128)(2,1)S(1)}, u32[]{:S(2)}, u32[]{:S(2)}) collective-permute-start(f16[80,256]{1,0:T(8,128)(2,1)S(1)} %pad_maximum_fusion.3), channel_id=1, source_target_pairs={{0,1},{1,0},{2,3},{3,2},{4,5},{5,4},{6,7},{7,6},{8,9},{9,8},{10,11... | collective-permute-start | bytes 122888 | tf_op jit(solution)/shard_map/ppermute | solution.py:57
  20.5 3.6 %collective-permute-start.6 = (f16[80,256]{1,0:T(8,128)(2,1)S(1)}, f16[80,256]{1,0:T(8,128)(2,1)S(1)}, u32[]{:S(2)}, u32[]{:S(2)}) collective-permute-start(f16[80,256]{1,0:T(8,128)(2,1)S(1)} %pad_maximum_fusion.7), channel_id=1, source_target_pairs={{0,10},{1,11},{2,8},{3,9},{4,14},{5,15},{6,12},{7,13},{8,2},{9,3},... | collective-permute-start | bytes 122888 | tf_op jit(solution)/shard_map/ppermute | solution.py:57
  22.0 4.5 %collective-permute-start.2 = (f16[80,256]{1,0:T(8,128)(2,1)S(1)}, f16[80,256]{1,0:T(8,128)(2,1)S(1)}, u32[]{:S(2)}, u32[]{:S(2)}) collective-permute-start(f16[80,256]{1,0:T(8,128)(2,1)S(1)} %pad_maximum_fusion.4), channel_id=1, source_target_pairs={{0,2},{1,3},{2,0},{3,1},{4,6},{5,7},{6,4},{7,5},{8,10},{9,11},{10,... | collective-permute-start | bytes 122888 | tf_op jit(solution)/shard_map/ppermute | solution.py:57
  24.3 4.8 %collective-permute-start.7 = (f16[80,256]{1,0:T(8,128)(2,1)S(1)}, f16[80,256]{1,0:T(8,128)(2,1)S(1)}, u32[]{:S(2)}, u32[]{:S(2)}) collective-permute-start(f16[80,256]{1,0:T(8,128)(2,1)S(1)} %pad_maximum_fusion.8), channel_id=1, source_target_pairs={{0,12},{1,13},{2,14},{3,15},{4,8},{5,9},{6,10},{7,11},{8,4},{9,5},... | collective-permute-start | bytes 122888 | tf_op jit(solution)/shard_map/ppermute | solution.py:57
  26.6 5.0 %collective-permute-start.3 = (f16[80,256]{1,0:T(8,128)(2,1)S(1)}, f16[80,256]{1,0:T(8,128)(2,1)S(1)}, u32[]{:S(2)}, u32[]{:S(2)}) collective-permute-start(f16[80,256]{1,0:T(8,128)(2,1)S(1)} %pad_maximum_fusion.5), channel_id=1, source_target_pairs={{0,4},{1,5},{2,6},{3,7},{4,0},{5,1},{6,2},{7,3},{8,12},{9,13},{10,... | collective-permute-start | bytes 122888 | tf_op jit(solution)/shard_map/ppermute | solution.py:57
  32.6 3.7 %collective-permute-start.8 = (f32[2,4096]{1,0:T(2,128)S(1)}, f32[2,4096]{1,0:T(2,128)S(1)}, u32[]{:S(2)}, u32[]{:S(2)}) collective-permute-start(f32[2,4096]{1,0:T(2,128)S(1)} %add.55), channel_id=1, source_target_pairs={{0,24},{1,25},{2,26},{3,27},{4,28},{5,29},{6,30},{7,31},{8,16},{9,... | collective-permute-start | bytes 98312 | tf_op jit(solution)/shard_map/ppermute | solution.py:57
  36.3 1.3 %collective-permute-start.9 = (f32[2,4096]{1,0:T(2,128)S(1)}, f32[2,4096]{1,0:T(2,128)S(1)}, u32[]{:S(2)}, u32[]{:S(2)}) collective-permute-start(f32[2,4096]{1,0:T(2,128)S(1)} %add.56), channel_id=1, source_target_pairs={{0,8},{1,9},{2,10},{3,11},{4,12},{5,13},{6,14},{7,15},{8,0},{9,1},... | collective-permute-start | bytes 98312 | tf_op jit(solution)/shard_map/ppermute | solution.py:57

commit v3 on v2

v3 whole, which is shorter than its diff:
```python
import jax
import jax.numpy as jnp
from jax import lax
from jax.experimental import pallas as pl
from jax.experimental.pallas import tpu as pltpu
from jax.sharding import PartitionSpec as P


HEADROOM = 14.0
TAG_ROWS = 8
SMALLEST = 2.0**-100


def power_of_two(n):
    return n & (n - 1) == 0


def fallback(src_fields, det_fields, probes):
    src_count, vox_count = src_fields.shape
    groups = lax.axis_size("blk")
    weighted = (src_fields.astype(jnp.float32)[None] * probes.astype(jnp.float32)[:, None]).astype(jnp.bfloat16)
    weighted = weighted.reshape(-1, vox_count)
    det_all = lax.all_gather(det_fields, "blk", axis=0, tiled=True)
    product = jnp.einsum("rv,dv->rd", weighted, det_all, preferred_element_type=jnp.float32)
    measured_b = lax.psum(product, "vox").astype(jnp.bfloat16)
    backproj = jnp.dot(measured_b, det_all, preferred_element_type=jnp.float32)
    backproj = backproj.reshape(-1, src_count, vox_count)
    contrib = jnp.sum(src_fields.astype(jnp.float32)[None] * backproj, axis=1)
    normalizer = jnp.float32(1.0 / (src_count * groups * det_all.shape[0]))
    return lax.psum(contrib, "blk") * normalizer


def pack(values, exponent):
    scaled = (values * jnp.exp2(HEADROOM - exponent)).astype(jnp.float16)
    tag = jnp.broadcast_to(exponent.astype(jnp.float16), (TAG_ROWS, values.shape[1]))
    return jnp.concatenate([scaled, tag], axis=0)


def unpack(packed):
    exponent = packed[-TAG_ROWS:][:1].astype(jnp.float32)
    return packed[:-TAG_ROWS].astype(jnp.float32) * jnp.exp2(exponent - HEADROOM), exponent


def stage(*arrays):
    count = len(arrays)

    def body(*refs):
        sources, targets, sems = refs[:count], refs[count : 2 * count], refs[2 * count]
        copies = [pltpu.make_async_copy(a, b, sems.at[i]) for i, (a, b) in enumerate(zip(sources, targets))]
        for copy in copies:
            copy.start()
        for copy in copies:
            copy.wait()

    return pl.pallas_call(
        body,
        out_shape=[pltpu.VMEM(a.shape, a.dtype) for a in arrays],
        in_specs=[pl.BlockSpec(memory_space=pl.ANY)] * count,
        out_specs=[pl.BlockSpec(memory_space=pltpu.VMEM)] * count,
        scratch_shapes=[pltpu.SemaphoreType.DMA((count,))],
        name="stage",
    )(*arrays)


def product(src_fields, det_fields, probes):
    src_count, vox_count = src_fields.shape
    det_count = det_fields.shape[0]
    probe_count = probes.shape[0]
    groups = lax.axis_size("blk")
    slabs = lax.axis_size("vox")
    chips = groups // 2
    if groups < 4 or slabs < 2 or not power_of_two(groups) or not power_of_two(slabs):
        return fallback(src_fields, det_fields, probes)

    def exchange(array, partner_of):
        pairs = []
        for b in range(groups):
            for u in range(slabs):
                partner = partner_of(b // 2, b % 2, u)
                if partner is not None:
                    chip, core, slab = partner
                    pairs.append((b * slabs + u, (2 * chip + core) * slabs + slab))
        return lax.ppermute(array, ("blk", "vox"), pairs)

    def core_swap(array):
        return exchange(array, lambda q, c, u: (q, c ^ 1, u))

    def fetch(array, j, trade):
        def partner_of(q, c, u):
            if c == 1:
                return q ^ (chips // 2 + j), c, u
            if j:
                return q ^ j, c, u
            return (q, c, u ^ 1) if trade else None

        return exchange(array, partner_of)

    south = (lax.axis_index("blk") & 1) == 0
    fetched_a = [fetch(det_fields, j, True) for j in range(chips // 2)]
    det_other = core_swap(det_fields)
    src_other = core_swap(src_fields)
    fetched_b = [fetch(det_other, j, False) for j in range(chips // 2)]
    src_fields, det_fields, probes = stage(src_fields, det_fields, probes)
    probe_rows = probes.astype(jnp.float32)[:, None]
    src = jnp.concatenate([src_fields, src_other], axis=0)
    weighted = (src.astype(jnp.float32)[None] * probe_rows).astype(jnp.bfloat16).reshape(-1, vox_count)

    dets, products = [], []
    for local, fetched in ((det_fields, fetched_a), (det_other, fetched_b)):
        for j, block in enumerate(fetched):
            det = block if j else jnp.where(south, local, block)
            dets.append(det)
            products.append(jnp.einsum("dv,rv->dr", det, weighted, preferred_element_type=jnp.float32))
    measured = jnp.concatenate(products, axis=0)

    exponent = jnp.ceil(jnp.log2(jnp.maximum(jnp.max(jnp.abs(measured), axis=0, keepdims=True), SMALLEST)))
    widths = [1 << i for i in range(slabs.bit_length() - 1)]
    for width in widths[-1:] + widths[:-1]:
        sent = exchange(pack(measured, exponent), lambda q, c, u, width=width: (q, c, u ^ width))
        received, other = unpack(sent)
        measured = measured + received
        exponent = jnp.maximum(exponent, other) + 1.0
    measured_b = measured.astype(jnp.bfloat16)

    total = jnp.zeros((probe_count, vox_count), jnp.float32)
    for i, det in enumerate(dets):
        rows = measured_b[i * det_count : (i + 1) * det_count].reshape(-1, probe_count, 2 * src_count)
        rows = rows.transpose(1, 0, 2).reshape(-1, 2 * src_count)
        back = jnp.dot(rows, src, preferred_element_type=jnp.float32).reshape(probe_count, -1, vox_count)
        total = total + jnp.sum(det.astype(jnp.float32)[None] * back, axis=1)
    total = total + core_swap(total)
    mask = 1
    while mask < chips:
        total = total + exchange(total, lambda q, c, u, mask=mask: (q ^ mask, c ^ 1, u))
        mask *= 2
    return total * jnp.float32(1.0 / (src_count * groups * det_count * groups))


def solution(mesh):
    return jax.shard_map(
        product,
        mesh=mesh,
        in_specs=(P("blk", "vox"), P("blk", "vox"), P(None, "vox")),
        out_specs=P(None, "vox"),
        check_vma=False,
    )
```

time: 38.5 us -> 33.8 us (0.88)
  waiting for transfers between devices: 17.4 us -> 13.2 us
  other arithmetic: 4.66 us -> 1.73 us
  Pallas kernels: 0 us -> 1.23 us
  starting transfers between devices: 12.8 us -> 13.7 us
  local copies, waits for them, and re-layouts: 0.73 us -> 1.14 us
    ppermute x10 -> x9, waiting for transfers between devices: 17.4 us -> 13.2 us  [exchange(): return lax.ppermute(array, ('blk', 'vox'), pairs)]
    pallas_call x0 -> x1, Pallas kernels: none -> 1.23 us  [stage(): pl.pallas_call(body, out_shape=[pltpu.VMEM(a.shape, a.dtype) for a in arr...]
    select_n x1 -> x0, other arithmetic: 1.12 us -> none  [product(): jnp.where(first, src_fields, partner)]
    concatenate x0 -> x1, local copies, waits for them, and re-layouts: none -> 1.08 us  [product(): src = jnp.concatenate([src_fields, src_other], axis=0)]
    convert_element_type x4 -> x5, other arithmetic: 1.76 us -> 0.77 us  [the longest x1 0.34 us: product(): (src.astype(jnp.float32)[None] * probe_rows).astype(jnp.bfloat16)]
    ppermute x10 -> x9, starting transfers between devices: 12.8 us -> 13.7 us  [exchange(): return lax.ppermute(array, ('blk', 'vox'), pairs)]
    convert_element_type x1, other arithmetic: 0.73 us -> 0.01 us  [product(): probe_rows = probes.astype(jnp.float32)[:, None]]
    unnamed x2, local copies, waits for them, and re-layouts: 0.69 us -> 0.04 us
  transfers between devices with their start and end apart: 10 -> 9, of which waited for: 7 -> 6; matrix products, arithmetic and copies ran while one was open for 12% -> 8% of each run, Pallas kernels for 0% -> 4%
where the time goes in v3:
time: 33.8 us; the launch traced here: 33.6 us
  starting transfers between devices  13.7 us (41%)
  waiting for transfers between devices  13.2 us (39%)
  matrix products  2.42 us (7%)
  other arithmetic  1.73 us (5%)
  Pallas kernels  1.23 us (4%)
  local copies, waits for them, and re-layouts  1.14 us (3%)
    ppermute x9, starting transfers between devices, exchange(): return lax.ppermute(array, ('blk', 'vox'), pairs)  13.7 us
    ppermute x9, waiting for transfers between devices, exchange(): return lax.ppermute(array, ('blk', 'vox'), pairs)  13.2 us
    dot_general x2, matrix products, product(): jnp.einsum('dv,rv->dr', det, weighted, preferred_element_type=jnp.float32)  1.53 us
    pallas_call x1, Pallas kernels, stage(): pl.pallas_call(body, out_shape=[pltpu.VMEM(a.shape, a.dtype) for a in arr...  1.23 us
    concatenate x1, local copies, waits for them, and re-layouts, product(): src = jnp.concatenate([src_fields, src_other], axis=0)  1.08 us
    dot_general x2, matrix products, product(): jnp.dot(rows, src, preferred_element_type=jnp.float32)  0.89 us
  transfers between devices with their start and end apart: 9, of which 6 were waited for; matrix products, arithmetic and copies ran while one was open for 8% of the time, Pallas kernels for 4%

profile of v3, /device:TPU:0, one launch (start us, length us, event | category | flops | bytes accessed | tf_op | source)
XLA Modules:
  0.0 33.6 jit_solution(17330632385341986958)
XLA Ops:
  0.0 0.5 %collective-permute-start.1 = (bf16[64,4096]{1,0:T(8,128)(2,1)}, bf16[64,4096]{1,0:T(8,128)(2,1)}, u32[]{:S(2)}, u32[]{:S(2)}) collective-permute-start(bf16[64,4096]{1,0:T(8,128)(2,1)} %refs_0_.1), channel_id=1, source_target_pairs={{0,8},{1,9},{2,10},{3,11},{4,12},{5,13},{6,14},{7,15},{8,0},{9,1},... | collective-permute-start | bytes 1572872 | tf_op jit(solution)/shard_map/ppermute | solution.py:83
  0.5 0.0 collective-permute-start.2
  0.5 3.0 %collective-permute-start = (bf16[64,4096]{1,0:T(8,128)(2,1)}, bf16[64,4096]{1,0:T(8,128)(2,1)S(1)}, u32[]{:S(2)}, u32[]{:S(2)}) collective-permute-start(bf16[64,4096]{1,0:T(8,128)(2,1)} %refs_1_.1), channel_id=1, source_target_pairs={{0,1},{1,0},{2,3},{3,2},{4,5},{5,4},{6,7},{7,6},{8,24},{9,25},{10,... | collective-permute-start | bytes 1572872 | tf_op jit(solution)/shard_map/ppermute | solution.py:83
  3.5 1.2 %stage.1 = (bf16[64,4096]{1,0:T(8,128)(2,1)S(1)}, bf16[64,4096]{1,0:T(8,128)(2,1)S(1)}, bf16[2,4096]{1,0:T(2,128)(2,1)S(1)}) custom-call(bf16[64,4096]{1,0:T(8,128)(2,1)} %refs_0_.1, bf16[64,4096]{1,0:T(8,128)(2,1)} %refs_1_.1, bf16[2,4096]{1,0:T(2,128)(2,1)} %refs_2_.1), custom_call_target="tpu_custom_call" | custom-call | tf_op jit(solution)/shard_map/stage/pallas_call | solution.py:55
  4.8 0.0 collective-permute-done.1
  4.8 1.1 %constant_dynamic-update-slice_fusion = bf16[128,4096]{1,0:T(8,128)(2,1)S(1)} fusion(bf16[128,4096]{1,0:T(8,128)(2,1)S(1)} %constant_dynamic-update-slice_fusion.1, bf16[64,4096]{1,0:T(8,128)(2,1)} %collective-permute-done.1), kind=kLoop, calls=%fused_computation.31 | loop fusion | bytes 1048576 | tf_op jit(solution)/shard_map/concatenate | solution.py:105
  5.9 0.2 convert_element_type.68
  6.1 0.0 collective-permute-done.2
  6.1 0.7 %collective-permute-start.3 = (bf16[64,4096]{1,0:T(8,128)(2,1)S(1)}, bf16[64,4096]{1,0:T(8,128)(2,1)S(1)}, u32[]{:S(2)}, u32[]{:S(2)}) collective-permute-start(bf16[64,4096]{1,0:T(8,128)(2,1)S(1)} %collective-permute-done.2), channel_id=1, source_target_pairs={{8,24},{9,25},{10,26},{11,27},{12,28},{13,29},{14,30},{15,31},{24,... | collective-permute-start | bytes 1572872 | tf_op jit(solution)/shard_map/ppermute | solution.py:83
  6.8 0.3 %multiply_convert_fusion = bf16[2,128,4096]{2,1,0:T(8,128)(2,1)S(1)} fusion(f32[2,4096]{1,0:T(2,128)S(1)} %convert_element_type.69, f32[128,4096]{1,0:T(8,128)S(1)} %convert_element_type.68), kind=kLoop, calls=%fused_computation | loop fusion | flops 2097152 | bytes 4227072 | tf_op jit(solution)/shard_map/convert_element_type | solution.py:106
  7.2 3.7 %collective-permute-done = bf16[64,4096]{1,0:T(8,128)(2,1)S(1)} collective-permute-done((bf16[64,4096]{1,0:T(8,128)(2,1)}, bf16[64,4096]{1,0:T(8,128)(2,1)S(1)}, u32[]{:S(2)}, u32[]{:S(2)}) %collective-permute-start) | collective-permute-done | bytes 524320 | tf_op jit(solution)/shard_map/ppermute | solution.py:83
  10.9 0.8 %fusion.4 = f32[64,256]{1,0:T(8,128)S(1)} fusion(bf16[256,4096]{1,0:T(8,128)(2,1)S(1)} %bitcast.42, bf16[64,4096]{1,0:T(8,128)(2,1)S(1)} %get-tuple-element.8, bf16[64,4096]{1,0:T(8,128)(2,1)S(1)} %collective-permute-done, pred[]{:T(512)S(6)} %eq.3), kind=kOutput, calls=%fused_computation.9 | convolution fusion | flops 134479872 | bytes 3211265 | tf_op jit(solution)/shard_map/dv,rv->dr/dot_general | solution.py:113
  11.6 0.0 collective-permute-done.3
  11.6 0.8 %fusion.7 = f32[64,256]{1,0:T(8,128)S(1)} fusion(bf16[256,4096]{1,0:T(8,128)(2,1)S(1)} %bitcast.43, bf16[64,4096]{1,0:T(8,128)(2,1)S(1)} %collective-permute-done.2, bf16[64,4096]{1,0:T(8,128)(2,1)S(1)} %collective-permute-done.3, pred[]{:T(512)S(6)} %eq.3), kind=kOutput, calls=%fused_computation.12 | convolution fusion | flops 134479872 | bytes 3211265 | tf_op jit(solution)/shard_map/dv,rv->dr/dot_general | solution.py:113
  12.5 3.2 %collective-permute-start.4 = (f16[136,256]{1,0:T(8,128)(2,1)S(1)}, f16[136,256]{1,0:T(8,128)(2,1)S(1)}, u32[]{:S(2)}, u32[]{:S(2)}) collective-permute-start(f16[136,256]{1,0:T(8,128)(2,1)S(1)} %pad_maximum_fusion.1), channel_id=1, source_target_pairs={{0,4},{1,5},{2,6},{3,7},{4,0},{5,1},{6,2},{7,3},{8,12},{9,13},{10,... | collective-permute-start | bytes 208904 | tf_op jit(solution)/shard_map/ppermute | solution.py:83
  15.7 2.3 %collective-permute-done.4 = f16[136,256]{1,0:T(8,128)(2,1)S(1)} collective-permute-done((f16[136,256]{1,0:T(8,128)(2,1)S(1)}, f16[136,256]{1,0:T(8,128)(2,1)S(1)}, u32[]{:S(2)}, u32[]{:S(2)}) %collective-permute-start.4) | collective-permute-done | bytes 69664 | tf_op jit(solution)/shard_map/ppermute | solution.py:83
  18.1 1.9 %collective-permute-start.5 = (f16[136,256]{1,0:T(8,128)(2,1)S(1)}, f16[136,256]{1,0:T(8,128)(2,1)S(1)}, u32[]{:S(2)}, u32[]{:S(2)}) collective-permute-start(f16[136,256]{1,0:T(8,128)(2,1)S(1)} %pad_maximum_fusion.2), channel_id=1, source_target_pairs={{0,1},{1,0},{2,3},{3,2},{4,5},{5,4},{6,7},{7,6},{8,9},{9,8},{10,11... | collective-permute-start | bytes 208904 | tf_op jit(solution)/shard_map/ppermute | solution.py:83
  20.0 0.1 fusion.5
  20.1 2.4 %collective-permute-done.5 = f16[136,256]{1,0:T(8,128)(2,1)S(1)} collective-permute-done((f16[136,256]{1,0:T(8,128)(2,1)S(1)}, f16[136,256]{1,0:T(8,128)(2,1)S(1)}, u32[]{:S(2)}, u32[]{:S(2)}) %collective-permute-start.5) | collective-permute-done | bytes 69664 | tf_op jit(solution)/shard_map/ppermute | solution.py:83
  22.6 2.0 %collective-permute-start.6 = (f16[136,256]{1,0:T(8,128)(2,1)S(1)}, f16[136,256]{1,0:T(8,128)(2,1)S(1)}, u32[]{:S(2)}, u32[]{:S(2)}) collective-permute-start(f16[136,256]{1,0:T(8,128)(2,1)S(1)} %pad_maximum_fusion.3), channel_id=1, source_target_pairs={{0,2},{1,3},{2,0},{3,1},{4,6},{5,7},{6,4},{7,5},{8,10},{9,11},{10,... | collective-permute-start | bytes 208904 | tf_op jit(solution)/shard_map/ppermute | solution.py:83
  24.6 0.1 fusion.6
  24.7 2.3 %collective-permute-done.6 = f16[136,256]{1,0:T(8,128)(2,1)S(1)} collective-permute-done((f16[136,256]{1,0:T(8,128)(2,1)S(1)}, f16[136,256]{1,0:T(8,128)(2,1)S(1)}, u32[]{:S(2)}, u32[]{:S(2)}) %collective-permute-start.6) | collective-permute-done | bytes 69664 | tf_op jit(solution)/shard_map/ppermute | solution.py:83
  27.0 0.1 add_convert_fusion
  27.1 0.4 %multiply_reduce_fusion = f32[2,4096]{1,0:T(2,128)S(1)} fusion(f32[64,4096]{1,0:T(8,128)S(1)} %fusion.6, bf16[128,4096]{1,0:T(8,128)(2,1)S(1)} %constant_dynamic-update-slice_fusion, bf16[8,2,8,128]{3,2,1,0:T(8,128)(2,1)S(1)} %get-tuple-element.17), kind=kOutput, calls=%fused_computation.1 | convolution fusion | flops 135258112 | bytes 2162688 | tf_op jit(solution)/shard_map/dot_general | solution.py:129
  27.5 0.4 %multiply_reduce_fusion.1 = f32[2,4096]{1,0:T(2,128)S(1)} fusion(f32[64,4096]{1,0:T(8,128)S(1)} %fusion.5, bf16[128,4096]{1,0:T(8,128)(2,1)S(1)} %constant_dynamic-update-slice_fusion, bf16[8,2,8,128]{3,2,1,0:T(8,128)(2,1)S(1)} %get-tuple-element.18), kind=kOutput, calls=%fused_computation.2 | convolution fusion | flops 135258112 | bytes 2162688 | tf_op jit(solution)/shard_map/dot_general | solution.py:129
  28.0 0.6 %collective-permute-start.7 = (f32[2,4096]{1,0:T(2,128)S(1)}, f32[2,4096]{1,0:T(2,128)S(1)}, u32[]{:S(2)}, u32[]{:S(2)}) collective-permute-start(f32[2,4096]{1,0:T(2,128)S(1)} %add.32), channel_id=1, source_target_pairs={{0,8},{1,9},{2,10},{3,11},{4,12},{5,13},{6,14},{7,15},{8,0},{9,1},... | collective-permute-start | bytes 98312 | tf_op jit(solution)/shard_map/ppermute | solution.py:83
  28.6 0.9 %collective-permute-done.7 = f32[2,4096]{1,0:T(2,128)S(1)} collective-permute-done((f32[2,4096]{1,0:T(2,128)S(1)}, f32[2,4096]{1,0:T(2,128)S(1)}, u32[]{:S(2)}, u32[]{:S(2)}) %collective-permute-start.7) | collective-permute-done | bytes 32800 | tf_op jit(solution)/shard_map/ppermute | solution.py:83
  29.5 1.8 %collective-permute-start.8 = (f32[2,4096]{1,0:T(2,128)S(1)}, f32[2,4096]{1,0:T(2,128)S(1)}, u32[]{:S(2)}, u32[]{:S(2)}) collective-permute-start(f32[2,4096]{1,0:T(2,128)S(1)} %add.33), channel_id=1, source_target_pairs={{0,24},{1,25},{2,26},{3,27},{4,28},{5,29},{6,30},{7,31},{8,16},{9,... | collective-permute-start | bytes 98312 | tf_op jit(solution)/shard_map/ppermute | solution.py:83
  31.3 1.6 %collective-permute-done.8 = f32[2,4096]{1,0:T(2,128)S(1)} collective-permute-done((f32[2,4096]{1,0:T(2,128)S(1)}, f32[2,4096]{1,0:T(2,128)S(1)}, u32[]{:S(2)}, u32[]{:S(2)}) %collective-permute-start.8) | collective-permute-done | bytes 32800 | tf_op jit(solution)/shard_map/ppermute | solution.py:83
  32.9 0.6 %add_multiply_fusion = f32[2,4096]{1,0:T(2,128)} fusion(f32[2,4096]{1,0:T(2,128)S(1)} %add.33, f32[2,4096]{1,0:T(2,128)S(1)} %collective-permute-done.8), kind=kLoop, calls=%fused_computation.30 | loop fusion | flops 16384 | bytes 98304 | tf_op jit(solution)/shard_map/mul | solution.py:136
  (21 shorter events, 0.4 us)
Async XLA Ops:
  0.0 4.8 %collective-permute-start.1 = (bf16[64,4096]{1,0:T(8,128)(2,1)}, bf16[64,4096]{1,0:T(8,128)(2,1)}, u32[]{:S(2)}, u32[]{:S(2)}) collective-permute-start(bf16[64,4096]{1,0:T(8,128)(2,1)} %refs_0_.1), channel_id=1, source_target_pairs={{0,8},{1,9},{2,10},{3,11},{4,12},{5,13},{6,14},{7,15},{8,0},{9,1},... | collective-permute-start | bytes 1572872 | tf_op jit(solution)/shard_map/ppermute | solution.py:83
  0.5 5.6 %collective-permute-start.2 = (bf16[64,4096]{1,0:T(8,128)(2,1)}, bf16[64,4096]{1,0:T(8,128)(2,1)S(1)}, u32[]{:S(2)}, u32[]{:S(2)}) collective-permute-start(bf16[64,4096]{1,0:T(8,128)(2,1)} %refs_1_.1), channel_id=1, source_target_pairs={{0,8},{1,9},{2,10},{3,11},{4,12},{5,13},{6,14},{7,15},{8,0},{9,1},... | collective-permute-start | bytes 1572872 | tf_op jit(solution)/shard_map/ppermute | solution.py:83
  0.5 10.4 %collective-permute-start = (bf16[64,4096]{1,0:T(8,128)(2,1)}, bf16[64,4096]{1,0:T(8,128)(2,1)S(1)}, u32[]{:S(2)}, u32[]{:S(2)}) collective-permute-start(bf16[64,4096]{1,0:T(8,128)(2,1)} %refs_1_.1), channel_id=1, source_target_pairs={{0,1},{1,0},{2,3},{3,2},{4,5},{5,4},{6,7},{7,6},{8,24},{9,25},{10,... | collective-permute-start | bytes 1572872 | tf_op jit(solution)/shard_map/ppermute | solution.py:83
  6.1 5.5 %collective-permute-start.3 = (bf16[64,4096]{1,0:T(8,128)(2,1)S(1)}, bf16[64,4096]{1,0:T(8,128)(2,1)S(1)}, u32[]{:S(2)}, u32[]{:S(2)}) collective-permute-start(bf16[64,4096]{1,0:T(8,128)(2,1)S(1)} %collective-permute-done.2), channel_id=1, source_target_pairs={{8,24},{9,25},{10,26},{11,27},{12,28},{13,29},{14,30},{15,31},{24,... | collective-permute-start | bytes 1572872 | tf_op jit(solution)/shard_map/ppermute | solution.py:83
  12.5 5.5 %collective-permute-start.4 = (f16[136,256]{1,0:T(8,128)(2,1)S(1)}, f16[136,256]{1,0:T(8,128)(2,1)S(1)}, u32[]{:S(2)}, u32[]{:S(2)}) collective-permute-start(f16[136,256]{1,0:T(8,128)(2,1)S(1)} %pad_maximum_fusion.1), channel_id=1, source_target_pairs={{0,4},{1,5},{2,6},{3,7},{4,0},{5,1},{6,2},{7,3},{8,12},{9,13},{10,... | collective-permute-start | bytes 208904 | tf_op jit(solution)/shard_map/ppermute | solution.py:83
  18.1 4.4 %collective-permute-start.5 = (f16[136,256]{1,0:T(8,128)(2,1)S(1)}, f16[136,256]{1,0:T(8,128)(2,1)S(1)}, u32[]{:S(2)}, u32[]{:S(2)}) collective-permute-start(f16[136,256]{1,0:T(8,128)(2,1)S(1)} %pad_maximum_fusion.2), channel_id=1, source_target_pairs={{0,1},{1,0},{2,3},{3,2},{4,5},{5,4},{6,7},{7,6},{8,9},{9,8},{10,11... | collective-permute-start | bytes 208904 | tf_op jit(solution)/shard_map/ppermute | solution.py:83
  22.6 4.4 %collective-permute-start.6 = (f16[136,256]{1,0:T(8,128)(2,1)S(1)}, f16[136,256]{1,0:T(8,128)(2,1)S(1)}, u32[]{:S(2)}, u32[]{:S(2)}) collective-permute-start(f16[136,256]{1,0:T(8,128)(2,1)S(1)} %pad_maximum_fusion.3), channel_id=1, source_target_pairs={{0,2},{1,3},{2,0},{3,1},{4,6},{5,7},{6,4},{7,5},{8,10},{9,11},{10,... | collective-permute-start | bytes 208904 | tf_op jit(solution)/shard_map/ppermute | solution.py:83
  28.0 1.5 %collective-permute-start.7 = (f32[2,4096]{1,0:T(2,128)S(1)}, f32[2,4096]{1,0:T(2,128)S(1)}, u32[]{:S(2)}, u32[]{:S(2)}) collective-permute-start(f32[2,4096]{1,0:T(2,128)S(1)} %add.32), channel_id=1, source_target_pairs={{0,8},{1,9},{2,10},{3,11},{4,12},{5,13},{6,14},{7,15},{8,0},{9,1},... | collective-permute-start | bytes 98312 | tf_op jit(solution)/shard_map/ppermute | solution.py:83
  29.5 3.4 %collective-permute-start.8 = (f32[2,4096]{1,0:T(2,128)S(1)}, f32[2,4096]{1,0:T(2,128)S(1)}, u32[]{:S(2)}, u32[]{:S(2)}) collective-permute-start(f32[2,4096]{1,0:T(2,128)S(1)} %add.33), channel_id=1, source_target_pairs={{0,24},{1,25},{2,26},{3,27},{4,28},{5,29},{6,30},{7,31},{8,16},{9,... | collective-permute-start | bytes 98312 | tf_op jit(solution)/shard_map/ppermute | solution.py:83

commit v4 on v3

--- a/solution.py
+++ b/solution.py
@@ -62,6 +62,29 @@
     )(*arrays)
 
 
+def choose_product(local_first, local, det, weighted):
+    def body(flag, local_ref, det_ref, weighted_ref, out_ref):
+        @pl.when(flag[0] == 1)
+        def _():
+            out_ref[...] = local_ref[...]
+
+        @pl.when(flag[0] == 0)
+        def _():
+            out_ref[...] = lax.dot_general(
+                det_ref[...], weighted_ref[...], (((1,), (1,)), ((), ())), preferred_element_type=jnp.float32
+            )
+
+    vmem = pl.BlockSpec(memory_space=pltpu.VMEM)
+    return pl.pallas_call(
+        body,
+        out_shape=pltpu.VMEM(local.shape, local.dtype),
+        in_specs=[pl.BlockSpec(memory_space=pltpu.SMEM), vmem, vmem, vmem],
+        out_specs=vmem,
+        compiler_params=pltpu.CompilerParams(vmem_limit_bytes=8 << 20),
+        name="choose_product",
+    )(local_first, *(pltpu.with_memory_space_constraint(x, pltpu.VMEM) for x in (local, det, weighted)))
+
+
 def product(src_fields, det_fields, probes):
     src_count, vox_count = src_fields.shape
     det_count = det_fields.shape[0]
@@ -105,12 +128,20 @@
     src = jnp.concatenate([src_fields, src_other], axis=0)
     weighted = (src.astype(jnp.float32)[None] * probe_rows).astype(jnp.bfloat16).reshape(-1, vox_count)
 
+    def measure(det):
+        return jnp.einsum("dv,rv->dr", det, weighted, preferred_element_type=jnp.float32)
+
+    flag = south.astype(jnp.int32).reshape(1)
     dets, products = [], []
     for local, fetched in ((det_fields, fetched_a), (det_other, fetched_b)):
+        local_product = measure(local)
         for j, block in enumerate(fetched):
-            det = block if j else jnp.where(south, local, block)
-            dets.append(det)
-            products.append(jnp.einsum("dv,rv->dr", det, weighted, preferred_element_type=jnp.float32))
+            if j:
+                dets.append(block)
+                products.append(measure(block))
+            else:
+                dets.append(jnp.where(south, local, block))
+                products.append(choose_product(flag, local_product, block, weighted))
     measured = jnp.concatenate(products, axis=0)
 
     exponent = jnp.ceil(jnp.log2(jnp.maximum(jnp.max(jnp.abs(measured), axis=0, keepdims=True), SMALLEST)))
@@ -128,11 +159,11 @@
         rows = rows.transpose(1, 0, 2).reshape(-1, 2 * src_count)
         back = jnp.dot(rows, src, preferred_element_type=jnp.float32).reshape(probe_count, -1, vox_count)
         total = total + jnp.sum(det.astype(jnp.float32)[None] * back, axis=1)
-    total = total + core_swap(total)
     mask = 1
     while mask < chips:
-        total = total + exchange(total, lambda q, c, u, mask=mask: (q ^ mask, c ^ 1, u))
+        total = total + exchange(total, lambda q, c, u, mask=mask: (q ^ mask, c, u))
         mask *= 2
+    total = total + core_swap(total)
     return total * jnp.float32(1.0 / (src_count * groups * det_count * groups))
 
 

time: 33.8 us -> 33.5 us (level)
  local copies, waits for them, and re-layouts: 1.14 us -> 0.1 us
  waiting for transfers between devices: 13.2 us -> 14.1 us
  starting transfers between devices: 13.7 us -> 13.3 us
    concatenate x1, local copies, waits for them, and re-layouts: 1.08 us -> 0.04 us  [product(): src = jnp.concatenate([src_fields, src_other], axis=0)]
    ppermute x9, waiting for transfers between devices: 13.2 us -> 14.1 us  [exchange(): return lax.ppermute(array, ('blk', 'vox'), pairs)]
    ppermute x9, starting transfers between devices: 13.7 us -> 13.3 us  [exchange(): return lax.ppermute(array, ('blk', 'vox'), pairs)]
  transfers between devices with their start and end apart: 9 -> 9, of which waited for: 6 -> 6; matrix products, arithmetic and copies ran while one was open for 8% -> 7% of each run, Pallas kernels for 4% -> 4%
where the time goes in v4:
time: 33.5 us; the launch traced here: 33.2 us
  waiting for transfers between devices  14.1 us (42%)
  starting transfers between devices  13.3 us (40%)
  matrix products  2.44 us (7%)
  other arithmetic  1.74 us (5%)
  Pallas kernels  1.25 us (4%)
    ppermute x9, waiting for transfers between devices, exchange(): return lax.ppermute(array, ('blk', 'vox'), pairs)  14.1 us
    ppermute x9, starting transfers between devices, exchange(): return lax.ppermute(array, ('blk', 'vox'), pairs)  13.3 us
    dot_general x2, matrix products, measure(): jnp.einsum('dv,rv->dr', det, weighted, preferred_element_type=jnp.float32)  1.52 us
    pallas_call x1, Pallas kernels, stage(): pl.pallas_call(body, out_shape=[pltpu.VMEM(a.shape, a.dtype) for a in arr...  1.23 us
    dot_general x2, matrix products, product(): jnp.dot(rows, src, preferred_element_type=jnp.float32)  0.92 us
  transfers between devices with their start and end apart: 9, of which 6 were waited for; matrix products, arithmetic and copies ran while one was open for 7% of the time, Pallas kernels for 4%

profile of v4, /device:TPU:0, one launch (start us, length us, event | category | flops | bytes accessed | tf_op | source)
XLA Modules:
  0.0 33.2 jit_solution(2147299819040320327)
XLA Ops:
  0.0 0.5 %collective-permute-start.1 = (bf16[64,4096]{1,0:T(8,128)(2,1)}, bf16[64,4096]{1,0:T(8,128)(2,1)S(1)}, u32[]{:S(2)}, u32[]{:S(2)}) collective-permute-start(bf16[64,4096]{1,0:T(8,128)(2,1)} %refs_0_.1), channel_id=1, source_target_pairs={{0,8},{1,9},{2,10},{3,11},{4,12},{5,13},{6,14},{7,15},{8,0},{9,1},... | collective-permute-start | bytes 1572872 | tf_op jit(solution)/shard_map/ppermute | solution.py:106
  0.5 0.0 collective-permute-start.2
  0.5 3.0 %collective-permute-start = (bf16[64,4096]{1,0:T(8,128)(2,1)}, bf16[64,4096]{1,0:T(8,128)(2,1)S(1)}, u32[]{:S(2)}, u32[]{:S(2)}) collective-permute-start(bf16[64,4096]{1,0:T(8,128)(2,1)} %refs_1_.1), channel_id=1, source_target_pairs={{0,1},{1,0},{2,3},{3,2},{4,5},{5,4},{6,7},{7,6},{8,24},{9,25},{10,... | collective-permute-start | bytes 1572872 | tf_op jit(solution)/shard_map/ppermute | solution.py:106
  3.5 1.2 %stage.1 = (bf16[64,4096]{1,0:T(8,128)(2,1)S(1)}, bf16[64,4096]{1,0:T(8,128)(2,1)S(1)}, bf16[2,4096]{1,0:T(2,128)(2,1)S(1)}) custom-call(bf16[64,4096]{1,0:T(8,128)(2,1)} %refs_0_.1, bf16[64,4096]{1,0:T(8,128)(2,1)} %refs_1_.1, bf16[2,4096]{1,0:T(2,128)(2,1)} %refs_2_.1), custom_call_target="tpu_custom_call" | custom-call | tf_op jit(solution)/shard_map/stage/pallas_call | solution.py:55
  4.8 0.0 collective-permute-done.1
  4.9 0.2 convert_element_type.69
  5.1 0.3 %multiply_convert_fusion = bf16[2,128,4096]{2,1,0:T(8,128)(2,1)S(1)} fusion(f32[2,4096]{1,0:T(2,128)S(1)} %convert_element_type.70, f32[128,4096]{1,0:T(8,128)S(1)} %convert_element_type.69), kind=kLoop, calls=%fused_computation | loop fusion | flops 2097152 | bytes 4227072 | tf_op jit(solution)/shard_map/convert_element_type | solution.py:129
  5.4 0.0 collective-permute-done.2
  5.4 0.7 %collective-permute-start.3 = (bf16[64,4096]{1,0:T(8,128)(2,1)S(1)}, bf16[64,4096]{1,0:T(8,128)(2,1)S(1)}, u32[]{:S(2)}, u32[]{:S(2)}) collective-permute-start(bf16[64,4096]{1,0:T(8,128)(2,1)S(1)} %collective-permute-done.2), channel_id=1, source_target_pairs={{8,24},{9,25},{10,26},{11,27},{12,28},{13,29},{14,30},{15,31},{24,... | collective-permute-start | bytes 1572872 | tf_op jit(solution)/shard_map/ppermute | solution.py:106
  6.1 0.8 %fusion.14.local_ref = f32[64,256]{1,0:T(8,128)S(1)} fusion(bf16[64,4096]{1,0:T(8,128)(2,1)S(1)} %get-tuple-element.8, bf16[256,4096]{1,0:T(8,128)(2,1)S(1)} %bitcast.47), kind=kOutput, calls=%fused_computation.47 | convolution fusion | flops 134217728 | bytes 2686976 | tf_op jit(solution)/shard_map/dv,rv->dr/dot_general | solution.py:132
  6.9 4.0 %collective-permute-done.det_ref = bf16[64,4096]{1,0:T(8,128)(2,1)S(1)} collective-permute-done((bf16[64,4096]{1,0:T(8,128)(2,1)}, bf16[64,4096]{1,0:T(8,128)(2,1)S(1)}, u32[]{:S(2)}, u32[]{:S(2)}) %collective-permute-start) | collective-permute-done | bytes 524320 | tf_op jit(solution)/shard_map/ppermute | solution.py:106
  10.9 0.8 %convolution_bitcast_fusion.local_ref = f32[64,256]{1,0:T(8,128)S(1)} fusion(bf16[256,4096]{1,0:T(8,128)(2,1)S(1)} %bitcast.49, bf16[64,4096]{1,0:T(8,128)(2,1)S(1)} %collective-permute-done.2), kind=kOutput, calls=%fused_computation.3 | convolution fusion | flops 134217728 | bytes 2686976 | tf_op jit(solution)/shard_map/dv,rv->dr/dot_general | solution.py:132
  11.6 0.0 collective-permute-done.3.det_ref
  11.8 3.2 %collective-permute-start.4 = (f16[136,256]{1,0:T(8,128)(2,1)S(1)}, f16[136,256]{1,0:T(8,128)(2,1)S(1)}, u32[]{:S(2)}, u32[]{:S(2)}) collective-permute-start(f16[136,256]{1,0:T(8,128)(2,1)S(1)} %pad_maximum_fusion.1), channel_id=1, source_target_pairs={{0,4},{1,5},{2,6},{3,7},{4,0},{5,1},{6,2},{7,3},{8,12},{9,13},{10,... | collective-permute-start | bytes 208904 | tf_op jit(solution)/shard_map/ppermute | solution.py:106
  14.9 2.3 %collective-permute-done.4 = f16[136,256]{1,0:T(8,128)(2,1)S(1)} collective-permute-done((f16[136,256]{1,0:T(8,128)(2,1)S(1)}, f16[136,256]{1,0:T(8,128)(2,1)S(1)}, u32[]{:S(2)}, u32[]{:S(2)}) %collective-permute-start.4) | collective-permute-done | bytes 69664 | tf_op jit(solution)/shard_map/ppermute | solution.py:106
  17.3 1.9 %collective-permute-start.5 = (f16[136,256]{1,0:T(8,128)(2,1)S(1)}, f16[136,256]{1,0:T(8,128)(2,1)S(1)}, u32[]{:S(2)}, u32[]{:S(2)}) collective-permute-start(f16[136,256]{1,0:T(8,128)(2,1)S(1)} %pad_maximum_fusion.2), channel_id=1, source_target_pairs={{0,1},{1,0},{2,3},{3,2},{4,5},{5,4},{6,7},{7,6},{8,9},{9,8},{10,11... | collective-permute-start | bytes 208904 | tf_op jit(solution)/shard_map/ppermute | solution.py:106
  19.3 0.1 select_convert_fusion.1
  19.3 2.4 %collective-permute-done.5 = f16[136,256]{1,0:T(8,128)(2,1)S(1)} collective-permute-done((f16[136,256]{1,0:T(8,128)(2,1)S(1)}, f16[136,256]{1,0:T(8,128)(2,1)S(1)}, u32[]{:S(2)}, u32[]{:S(2)}) %collective-permute-start.5) | collective-permute-done | bytes 69664 | tf_op jit(solution)/shard_map/ppermute | solution.py:106
  21.9 2.0 %collective-permute-start.6 = (f16[136,256]{1,0:T(8,128)(2,1)S(1)}, f16[136,256]{1,0:T(8,128)(2,1)S(1)}, u32[]{:S(2)}, u32[]{:S(2)}) collective-permute-start(f16[136,256]{1,0:T(8,128)(2,1)S(1)} %pad_maximum_fusion.3), channel_id=1, source_target_pairs={{0,2},{1,3},{2,0},{3,1},{4,6},{5,7},{6,4},{7,5},{8,10},{9,11},{10,... | collective-permute-start | bytes 208904 | tf_op jit(solution)/shard_map/ppermute | solution.py:106
  23.8 0.1 select_convert_fusion
  23.9 2.3 %collective-permute-done.6 = f16[136,256]{1,0:T(8,128)(2,1)S(1)} collective-permute-done((f16[136,256]{1,0:T(8,128)(2,1)S(1)}, f16[136,256]{1,0:T(8,128)(2,1)S(1)}, u32[]{:S(2)}, u32[]{:S(2)}) %collective-permute-start.6) | collective-permute-done | bytes 69664 | tf_op jit(solution)/shard_map/ppermute | solution.py:106
  26.2 0.1 add_convert_fusion
  26.3 0.5 %multiply_reduce_fusion = f32[2,4096]{1,0:T(2,128)S(1)} fusion(f32[64,4096]{1,0:T(8,128)S(1)} %select_convert_fusion, bf16[128,4096]{1,0:T(8,128)(2,1)S(1)} %constant_dynamic-update-slice_fusion, bf16[8,2,8,128]{3,2,1,0:T(8,128)(2,1)S(1)} %get-tuple-element.17), kind=kOutput, calls=%fused_computation.1 | convolution fusion | flops 135258112 | bytes 2162688 | tf_op jit(solution)/shard_map/dot_general | solution.py:160
  26.8 0.5 %multiply_reduce_fusion.1 = f32[2,4096]{1,0:T(2,128)S(1)} fusion(f32[64,4096]{1,0:T(8,128)S(1)} %select_convert_fusion.1, bf16[128,4096]{1,0:T(8,128)(2,1)S(1)} %constant_dynamic-update-slice_fusion, bf16[8,2,8,128]{3,2,1,0:T(8,128)(2,1)S(1)} %get-tuple-element.18), kind=kOutput, calls=%fused_computation.2 | convolution fusion | flops 135258112 | bytes 2162688 | tf_op jit(solution)/shard_map/dot_general | solution.py:160
  27.3 1.9 %collective-permute-start.7 = (f32[2,4096]{1,0:T(2,128)S(1)}, f32[2,4096]{1,0:T(2,128)S(1)}, u32[]{:S(2)}, u32[]{:S(2)}) collective-permute-start(f32[2,4096]{1,0:T(2,128)S(1)} %add.32), channel_id=1, source_target_pairs={{0,16},{1,17},{2,18},{3,19},{4,20},{5,21},{6,22},{7,23},{8,24},{9,... | collective-permute-start | bytes 98312 | tf_op jit(solution)/shard_map/ppermute | solution.py:106
  29.2 2.1 %collective-permute-done.7 = f32[2,4096]{1,0:T(2,128)S(1)} collective-permute-done((f32[2,4096]{1,0:T(2,128)S(1)}, f32[2,4096]{1,0:T(2,128)S(1)}, u32[]{:S(2)}, u32[]{:S(2)}) %collective-permute-start.7) | collective-permute-done | bytes 32800 | tf_op jit(solution)/shard_map/ppermute | solution.py:106
  31.3 0.2 collective-permute-start.8
  31.5 1.1 %collective-permute-done.8 = f32[2,4096]{1,0:T(2,128)S(1)} collective-permute-done((f32[2,4096]{1,0:T(2,128)S(1)}, f32[2,4096]{1,0:T(2,128)S(1)}, u32[]{:S(2)}, u32[]{:S(2)}) %collective-permute-start.8) | collective-permute-done | bytes 32800 | tf_op jit(solution)/shard_map/ppermute | solution.py:106
  32.6 0.6 %add_multiply_fusion = f32[2,4096]{1,0:T(2,128)} fusion(f32[2,4096]{1,0:T(2,128)S(1)} %add.33, f32[2,4096]{1,0:T(2,128)S(1)} %collective-permute-done.8), kind=kLoop, calls=%fused_computation.27 | loop fusion | flops 16384 | bytes 98304 | tf_op jit(solution)/shard_map/mul | solution.py:167
  (24 shorter events, 0.4 us)
Async XLA Ops:
  0.0 4.8 %collective-permute-start.1 = (bf16[64,4096]{1,0:T(8,128)(2,1)}, bf16[64,4096]{1,0:T(8,128)(2,1)S(1)}, u32[]{:S(2)}, u32[]{:S(2)}) collective-permute-start(bf16[64,4096]{1,0:T(8,128)(2,1)} %refs_0_.1), channel_id=1, source_target_pairs={{0,8},{1,9},{2,10},{3,11},{4,12},{5,13},{6,14},{7,15},{8,0},{9,1},... | collective-permute-start | bytes 1572872 | tf_op jit(solution)/shard_map/ppermute | solution.py:106
  0.5 4.9 %collective-permute-start.2 = (bf16[64,4096]{1,0:T(8,128)(2,1)}, bf16[64,4096]{1,0:T(8,128)(2,1)S(1)}, u32[]{:S(2)}, u32[]{:S(2)}) collective-permute-start(bf16[64,4096]{1,0:T(8,128)(2,1)} %refs_1_.1), channel_id=1, source_target_pairs={{0,8},{1,9},{2,10},{3,11},{4,12},{5,13},{6,14},{7,15},{8,0},{9,1},... | collective-permute-start | bytes 1572872 | tf_op jit(solution)/shard_map/ppermute | solution.py:106
  0.5 10.4 %collective-permute-start = (bf16[64,4096]{1,0:T(8,128)(2,1)}, bf16[64,4096]{1,0:T(8,128)(2,1)S(1)}, u32[]{:S(2)}, u32[]{:S(2)}) collective-permute-start(bf16[64,4096]{1,0:T(8,128)(2,1)} %refs_1_.1), channel_id=1, source_target_pairs={{0,1},{1,0},{2,3},{3,2},{4,5},{5,4},{6,7},{7,6},{8,24},{9,25},{10,... | collective-permute-start | bytes 1572872 | tf_op jit(solution)/shard_map/ppermute | solution.py:106
  5.4 6.2 %collective-permute-start.3 = (bf16[64,4096]{1,0:T(8,128)(2,1)S(1)}, bf16[64,4096]{1,0:T(8,128)(2,1)S(1)}, u32[]{:S(2)}, u32[]{:S(2)}) collective-permute-start(bf16[64,4096]{1,0:T(8,128)(2,1)S(1)} %collective-permute-done.2), channel_id=1, source_target_pairs={{8,24},{9,25},{10,26},{11,27},{12,28},{13,29},{14,30},{15,31},{24,... | collective-permute-start | bytes 1572872 | tf_op jit(solution)/shard_map/ppermute | solution.py:106
  11.8 5.4 %collective-permute-start.4 = (f16[136,256]{1,0:T(8,128)(2,1)S(1)}, f16[136,256]{1,0:T(8,128)(2,1)S(1)}, u32[]{:S(2)}, u32[]{:S(2)}) collective-permute-start(f16[136,256]{1,0:T(8,128)(2,1)S(1)} %pad_maximum_fusion.1), channel_id=1, source_target_pairs={{0,4},{1,5},{2,6},{3,7},{4,0},{5,1},{6,2},{7,3},{8,12},{9,13},{10,... | collective-permute-start | bytes 208904 | tf_op jit(solution)/shard_map/ppermute | solution.py:106
  17.3 4.4 %collective-permute-start.5 = (f16[136,256]{1,0:T(8,128)(2,1)S(1)}, f16[136,256]{1,0:T(8,128)(2,1)S(1)}, u32[]{:S(2)}, u32[]{:S(2)}) collective-permute-start(f16[136,256]{1,0:T(8,128)(2,1)S(1)} %pad_maximum_fusion.2), channel_id=1, source_target_pairs={{0,1},{1,0},{2,3},{3,2},{4,5},{5,4},{6,7},{7,6},{8,9},{9,8},{10,11... | collective-permute-start | bytes 208904 | tf_op jit(solution)/shard_map/ppermute | solution.py:106
  21.9 4.4 %collective-permute-start.6 = (f16[136,256]{1,0:T(8,128)(2,1)S(1)}, f16[136,256]{1,0:T(8,128)(2,1)S(1)}, u32[]{:S(2)}, u32[]{:S(2)}) collective-permute-start(f16[136,256]{1,0:T(8,128)(2,1)S(1)} %pad_maximum_fusion.3), channel_id=1, source_target_pairs={{0,2},{1,3},{2,0},{3,1},{4,6},{5,7},{6,4},{7,5},{8,10},{9,11},{10,... | collective-permute-start | bytes 208904 | tf_op jit(solution)/shard_map/ppermute | solution.py:106
  27.3 4.0 %collective-permute-start.7 = (f32[2,4096]{1,0:T(2,128)S(1)}, f32[2,4096]{1,0:T(2,128)S(1)}, u32[]{:S(2)}, u32[]{:S(2)}) collective-permute-start(f32[2,4096]{1,0:T(2,128)S(1)} %add.32), channel_id=1, source_target_pairs={{0,16},{1,17},{2,18},{3,19},{4,20},{5,21},{6,22},{7,23},{8,24},{9,... | collective-permute-start | bytes 98312 | tf_op jit(solution)/shard_map/ppermute | solution.py:106
  31.3 1.3 %collective-permute-start.8 = (f32[2,4096]{1,0:T(2,128)S(1)}, f32[2,4096]{1,0:T(2,128)S(1)}, u32[]{:S(2)}, u32[]{:S(2)}) collective-permute-start(f32[2,4096]{1,0:T(2,128)S(1)} %add.33), channel_id=1, source_target_pairs={{0,8},{1,9},{2,10},{3,11},{4,12},{5,13},{6,14},{7,15},{8,0},{9,1},... | collective-permute-start | bytes 98312 | tf_op jit(solution)/shard_map/ppermute | solution.py:106

commit v5 on v4

--- a/solution.py
+++ b/solution.py
@@ -9,6 +9,7 @@
 HEADROOM = 14.0
 TAG_ROWS = 8
 SMALLEST = 2.0**-100
+CHUNK = 512
 
 
 def power_of_two(n):
@@ -62,6 +63,35 @@
     )(*arrays)
 
 
+def in_vmem(body, shape, dtype, *arrays, flags=()):
+    vmem = pl.BlockSpec(memory_space=pltpu.VMEM)
+    return pl.pallas_call(
+        body,
+        out_shape=pltpu.VMEM(shape, dtype),
+        in_specs=[pl.BlockSpec(memory_space=pltpu.SMEM)] * len(flags) + [vmem] * len(arrays),
+        out_specs=vmem,
+        compiler_params=pltpu.CompilerParams(vmem_limit_bytes=16 << 20),
+    )(*flags, *(pltpu.with_memory_space_constraint(x, pltpu.VMEM) for x in arrays))
+
+
+def chunks(extent):
+    size = min(extent, CHUNK)
+    return [slice(i, min(i + size, extent)) for i in range(0, extent, size)]
+
+
+def weigh(src, probes):
+    count, extent = src.shape
+
+    def body(src_ref, probes_ref, out_ref):
+        for cut in chunks(extent):
+            values = src_ref[:, cut].astype(jnp.float32)
+            for k in range(probes.shape[0]):
+                weighted = (values * probes_ref[k : k + 1, cut].astype(jnp.float32)).astype(jnp.bfloat16)
+                out_ref[cut, k * count : (k + 1) * count] = weighted.T
+
+    return in_vmem(body, (extent, probes.shape[0] * count), jnp.bfloat16, src, probes)
+
+
 def choose_product(local_first, local, det, weighted):
     def body(flag, local_ref, det_ref, weighted_ref, out_ref):
         @pl.when(flag[0] == 1)
@@ -70,23 +100,34 @@
 
         @pl.when(flag[0] == 0)
         def _():
-            out_ref[...] = lax.dot_general(
-                det_ref[...], weighted_ref[...], (((1,), (1,)), ((), ())), preferred_element_type=jnp.float32
-            )
-
-    vmem = pl.BlockSpec(memory_space=pltpu.VMEM)
-    return pl.pallas_call(
-        body,
-        out_shape=pltpu.VMEM(local.shape, local.dtype),
-        in_specs=[pl.BlockSpec(memory_space=pltpu.SMEM), vmem, vmem, vmem],
-        out_specs=vmem,
-        compiler_params=pltpu.CompilerParams(vmem_limit_bytes=8 << 20),
-        name="choose_product",
-    )(local_first, *(pltpu.with_memory_space_constraint(x, pltpu.VMEM) for x in (local, det, weighted)))
+            out_ref[...] = jnp.dot(det_ref[...], weighted_ref[...], preferred_element_type=jnp.float32)
+
+    return in_vmem(body, local.shape, local.dtype, local, det, weighted, flags=(local_first,))
+
+
+def project(measured_b, src, dets, probe_count):
+    count, extent = src.shape
+
+    def body(measured_ref, src_ref, *refs):
+        det_refs, out_ref = refs[:-1], refs[-1]
+        rows = [measured_ref[:, k * count : (k + 1) * count] for k in range(probe_count)]
+        rows = jnp.concatenate(rows, axis=0)
+        for cut in chunks(extent):
+            back = jnp.dot(rows, src_ref[:, cut], preferred_element_type=jnp.float32)
+            first = 0
+            for k in range(probe_count):
+                total = 0.0
+                for det_ref in det_refs:
+                    last = first + det_ref.shape[0]
+                    total = total + jnp.sum(back[first:last] * det_ref[:, cut].astype(jnp.float32), axis=0, keepdims=True)
+                    first = last
+                out_ref[k : k + 1, cut] = total
+
+    return in_vmem(body, (probe_count, extent), jnp.float32, measured_b, src, *dets)
 
 
 def product(src_fields, det_fields, probes):
-    src_count, vox_count = src_fields.shape
+    src_count, _ = src_fields.shape
     det_count = det_fields.shape[0]
     probe_count = probes.shape[0]
     groups = lax.axis_size("blk")
@@ -124,12 +165,11 @@
     src_other = core_swap(src_fields)
     fetched_b = [fetch(det_other, j, False) for j in range(chips // 2)]
     src_fields, det_fields, probes = stage(src_fields, det_fields, probes)
-    probe_rows = probes.astype(jnp.float32)[:, None]
     src = jnp.concatenate([src_fields, src_other], axis=0)
-    weighted = (src.astype(jnp.float32)[None] * probe_rows).astype(jnp.bfloat16).reshape(-1, vox_count)
+    weighted = weigh(src, probes)
 
     def measure(det):
-        return jnp.einsum("dv,rv->dr", det, weighted, preferred_element_type=jnp.float32)
+        return jnp.dot(det, weighted, preferred_element_type=jnp.float32)
 
     flag = south.astype(jnp.int32).reshape(1)
     dets, products = [], []
@@ -153,12 +193,7 @@
         exponent = jnp.maximum(exponent, other) + 1.0
     measured_b = measured.astype(jnp.bfloat16)
 
-    total = jnp.zeros((probe_count, vox_count), jnp.float32)
-    for i, det in enumerate(dets):
-        rows = measured_b[i * det_count : (i + 1) * det_count].reshape(-1, probe_count, 2 * src_count)
-        rows = rows.transpose(1, 0, 2).reshape(-1, 2 * src_count)
-        back = jnp.dot(rows, src, preferred_element_type=jnp.float32).reshape(probe_count, -1, vox_count)
-        total = total + jnp.sum(det.astype(jnp.float32)[None] * back, axis=1)
+    total = project(measured_b, src, dets, probe_count)
     mask = 1
     while mask < chips:
         total = total + exchange(total, lambda q, c, u, mask=mask: (q ^ mask, c, u))

time: 33.5 us -> 33.3 us (level)
  matrix products: 2.44 us -> 0.93 us
  Pallas kernels: 1.25 us -> 2.61 us
  local copies, waits for them, and re-layouts: 0.1 us -> 1.14 us
  waiting for transfers between devices: 14.1 us -> 13.2 us
  starting transfers between devices: 13.3 us -> 14 us
  other arithmetic: 1.74 us -> 1.1 us
    dot_general x4 -> x2, matrix products: 2.44 us -> 0.93 us  [measure(): return jnp.dot(det, weighted, preferred_element_type=jnp.float32)]
    pallas_call x2 -> x4, Pallas kernels: 0.02 us -> 1.38 us  [in_vmem(): pl.pallas_call(body, out_shape=pltpu.VMEM(shape, dtype), in_specs=[pl.Blo...]
    concatenate x1, local copies, waits for them, and re-layouts: 0.04 us -> 1.08 us  [product(): src = jnp.concatenate([src_fields, src_other], axis=0)]
    ppermute x9, waiting for transfers between devices: 14.1 us -> 13.2 us  [exchange(): return lax.ppermute(array, ('blk', 'vox'), pairs)]
    convert_element_type x5 -> x0, other arithmetic: 0.74 us -> none  [the longest x1 0.34 us: product(): (src.astype(jnp.float32)[None] * probe_rows).astype(jnp.bfloat16)]
    ppermute x9, starting transfers between devices: 13.3 us -> 14 us  [exchange(): return lax.ppermute(array, ('blk', 'vox'), pairs)]
  transfers between devices with their start and end apart: 9 -> 9, of which waited for: 6 -> 6; matrix products, arithmetic and copies ran while one was open for 7% -> 7% of each run, Pallas kernels for 4% -> 6%
where the time goes in v5:
time: 33.3 us; the launch traced here: 33.1 us
  starting transfers between devices  14 us (42%)
  waiting for transfers between devices  13.2 us (40%)
  Pallas kernels  2.61 us (8%)
  local copies, waits for them, and re-layouts  1.14 us (3%)
  other arithmetic  1.1 us (3%)
  matrix products  0.93 us (3%)
    ppermute x9, starting transfers between devices, exchange(): return lax.ppermute(array, ('blk', 'vox'), pairs)  14 us
    ppermute x9, waiting for transfers between devices, exchange(): return lax.ppermute(array, ('blk', 'vox'), pairs)  13.2 us
    pallas_call x4, Pallas kernels, in_vmem(): pl.pallas_call(body, out_shape=pltpu.VMEM(shape, dtype), in_specs=[pl.Blo...  1.38 us
    pallas_call x1, Pallas kernels, stage(): pl.pallas_call(body, out_shape=[pltpu.VMEM(a.shape, a.dtype) for a in arr...  1.23 us
    concatenate x1, local copies, waits for them, and re-layouts, product(): src = jnp.concatenate([src_fields, src_other], axis=0)  1.08 us
    dot_general x2, matrix products, measure(): return jnp.dot(det, weighted, preferred_element_type=jnp.float32)  0.93 us
  transfers between devices with their start and end apart: 9, of which 6 were waited for; matrix products, arithmetic and copies ran while one was open for 7% of the time, Pallas kernels for 6%

profile of v5, /device:TPU:0, one launch (start us, length us, event | category | flops | bytes accessed | tf_op | source)
XLA Modules:
  0.0 33.1 jit_solution(13825815150634521663)
XLA Ops:
  0.0 0.5 %collective-permute-start = (bf16[64,4096]{1,0:T(8,128)(2,1)}, bf16[64,4096]{1,0:T(8,128)(2,1)}, u32[]{:S(2)}, u32[]{:S(2)}) collective-permute-start(bf16[64,4096]{1,0:T(8,128)(2,1)} %refs_0_.1), channel_id=1, source_target_pairs={{0,8},{1,9},{2,10},{3,11},{4,12},{5,13},{6,14},{7,15},{8,0},{9,1},... | collective-permute-start | bytes 1572872 | tf_op jit(solution)/shard_map/ppermute | solution.py:147
  0.5 0.0 collective-permute-start.2
  0.5 3.0 %collective-permute-start.1 = (bf16[64,4096]{1,0:T(8,128)(2,1)}, bf16[64,4096]{1,0:T(8,128)(2,1)S(1)}, u32[]{:S(2)}, u32[]{:S(2)}) collective-permute-start(bf16[64,4096]{1,0:T(8,128)(2,1)} %refs_1_.1), channel_id=1, source_target_pairs={{0,1},{1,0},{2,3},{3,2},{4,5},{5,4},{6,7},{7,6},{8,24},{9,25},{10,... | collective-permute-start | bytes 1572872 | tf_op jit(solution)/shard_map/ppermute | solution.py:147
  3.5 1.2 %stage.1 = (bf16[64,4096]{1,0:T(8,128)(2,1)S(1)}, bf16[64,4096]{1,0:T(8,128)(2,1)S(1)}, bf16[2,4096]{1,0:T(2,128)(2,1)S(1)}) custom-call(bf16[64,4096]{1,0:T(8,128)(2,1)} %refs_0_.1, bf16[64,4096]{1,0:T(8,128)(2,1)} %refs_1_.1, bf16[2,4096]{1,0:T(2,128)(2,1)} %refs_2_.1), custom_call_target="tpu_custom_call" | custom-call | tf_op jit(solution)/shard_map/stage/pallas_call | solution.py:56
  4.8 0.0 collective-permute-done
  4.8 1.1 %constant_dynamic-update-slice_fusion.src_ref = bf16[128,4096]{1,0:T(8,128)(2,1)S(1)} fusion(bf16[128,4096]{1,0:T(8,128)(2,1)S(1)} %constant_dynamic-update-slice_fusion.1, bf16[64,4096]{1,0:T(8,128)(2,1)} %collective-permute-done), kind=kLoop, calls=%fused_computation.15 | loop fusion | bytes 1048576 | tf_op jit(solution)/shard_map/concatenate | solution.py:168
  5.9 0.6 %shard_map.37.weighted_ref = bf16[4096,256]{1,0:T(8,128)(2,1)S(1)} custom-call(bf16[128,4096]{1,0:T(8,128)(2,1)S(1)} %constant_dynamic-update-slice_fusion.src_ref, bf16[2,4096]{1,0:T(2,128)(2,1)S(1)} %get-tuple-element.10.probes_ref), custom_call_target="tpu_custom_call" | custom-call | tf_op jit(solution)/shard_map/pallas_call | solution.py:68
  6.5 0.0 collective-permute-done.2
  6.5 0.7 %collective-permute-start.3 = (bf16[64,4096]{1,0:T(8,128)(2,1)S(1)}, bf16[64,4096]{1,0:T(8,128)(2,1)S(1)}, u32[]{:S(2)}, u32[]{:S(2)}) collective-permute-start(bf16[64,4096]{1,0:T(8,128)(2,1)S(1)} %collective-permute-done.2), channel_id=1, source_target_pairs={{8,24},{9,25},{10,26},{11,27},{12,28},{13,29},{14,30},{15,31},{24,... | collective-permute-start | bytes 1572872 | tf_op jit(solution)/shard_map/ppermute | solution.py:147
  7.2 0.5 %fusion.4.local_ref = f32[64,256]{1,0:T(8,128)S(1)} fusion(bf16[64,4096]{1,0:T(8,128)(2,1)S(1)} %get-tuple-element.8, bf16[4096,256]{1,0:T(8,128)(2,1)S(1)} %shard_map.37.weighted_ref), kind=kOutput, calls=%fused_computation.34 | convolution fusion | flops 134217728 | bytes 2686976 | tf_op jit(solution)/shard_map/dot_general | solution.py:172
  7.7 3.2 %collective-permute-done.1.det_ref = bf16[64,4096]{1,0:T(8,128)(2,1)S(1)} collective-permute-done((bf16[64,4096]{1,0:T(8,128)(2,1)}, bf16[64,4096]{1,0:T(8,128)(2,1)S(1)}, u32[]{:S(2)}, u32[]{:S(2)}) %collective-permute-start.1) | collective-permute-done | bytes 524320 | tf_op jit(solution)/shard_map/ppermute | solution.py:147
  10.9 0.5 %convolution_bitcast_fusion.local_ref = f32[64,256]{1,0:T(8,128)S(1)} fusion(bf16[64,4096]{1,0:T(8,128)(2,1)S(1)} %collective-permute-done.2, bf16[4096,256]{1,0:T(8,128)(2,1)S(1)} %shard_map.37.weighted_ref), kind=kOutput, calls=%fused_computation | convolution fusion | flops 134217728 | bytes 2686976 | tf_op jit(solution)/shard_map/dot_general | solution.py:172
  11.4 0.0 collective-permute-done.3.det_ref
  11.5 3.2 %collective-permute-start.4 = (f16[136,256]{1,0:T(8,128)(2,1)S(1)}, f16[136,256]{1,0:T(8,128)(2,1)S(1)}, u32[]{:S(2)}, u32[]{:S(2)}) collective-permute-start(f16[136,256]{1,0:T(8,128)(2,1)S(1)} %pad_maximum_fusion.1), channel_id=1, source_target_pairs={{0,4},{1,5},{2,6},{3,7},{4,0},{5,1},{6,2},{7,3},{8,12},{9,13},{10,... | collective-permute-start | bytes 208904 | tf_op jit(solution)/shard_map/ppermute | solution.py:147
  14.7 2.3 %collective-permute-done.4 = f16[136,256]{1,0:T(8,128)(2,1)S(1)} collective-permute-done((f16[136,256]{1,0:T(8,128)(2,1)S(1)}, f16[136,256]{1,0:T(8,128)(2,1)S(1)}, u32[]{:S(2)}, u32[]{:S(2)}) %collective-permute-start.4) | collective-permute-done | bytes 69664 | tf_op jit(solution)/shard_map/ppermute | solution.py:147
  17.1 1.9 %collective-permute-start.5 = (f16[136,256]{1,0:T(8,128)(2,1)S(1)}, f16[136,256]{1,0:T(8,128)(2,1)S(1)}, u32[]{:S(2)}, u32[]{:S(2)}) collective-permute-start(f16[136,256]{1,0:T(8,128)(2,1)S(1)} %pad_maximum_fusion.2), channel_id=1, source_target_pairs={{0,1},{1,0},{2,3},{3,2},{4,5},{5,4},{6,7},{7,6},{8,9},{9,8},{10,11... | collective-permute-start | bytes 208904 | tf_op jit(solution)/shard_map/ppermute | solution.py:147
  19.0 0.1 broadcast_select_fusion.1.refs_0_
  19.0 2.4 %collective-permute-done.5 = f16[136,256]{1,0:T(8,128)(2,1)S(1)} collective-permute-done((f16[136,256]{1,0:T(8,128)(2,1)S(1)}, f16[136,256]{1,0:T(8,128)(2,1)S(1)}, u32[]{:S(2)}, u32[]{:S(2)}) %collective-permute-start.5) | collective-permute-done | bytes 69664 | tf_op jit(solution)/shard_map/ppermute | solution.py:147
  21.6 2.0 %collective-permute-start.6 = (f16[136,256]{1,0:T(8,128)(2,1)S(1)}, f16[136,256]{1,0:T(8,128)(2,1)S(1)}, u32[]{:S(2)}, u32[]{:S(2)}) collective-permute-start(f16[136,256]{1,0:T(8,128)(2,1)S(1)} %pad_maximum_fusion.3), channel_id=1, source_target_pairs={{0,2},{1,3},{2,0},{3,1},{4,6},{5,7},{6,4},{7,5},{8,10},{9,11},{10,... | collective-permute-start | bytes 208904 | tf_op jit(solution)/shard_map/ppermute | solution.py:147
  23.5 0.1 broadcast_select_fusion.refs_1_
  23.6 2.3 %collective-permute-done.6 = f16[136,256]{1,0:T(8,128)(2,1)S(1)} collective-permute-done((f16[136,256]{1,0:T(8,128)(2,1)S(1)}, f16[136,256]{1,0:T(8,128)(2,1)S(1)}, u32[]{:S(2)}, u32[]{:S(2)}) %collective-permute-start.6) | collective-permute-done | bytes 69664 | tf_op jit(solution)/shard_map/ppermute | solution.py:147
  26.0 0.1 add_convert_fusion.measured_ref
  26.0 0.7 %shard_map.40 = f32[2,4096]{1,0:T(2,128)S(1)} custom-call(bf16[128,256]{1,0:T(8,128)(2,1)S(1)} %add_convert_fusion.measured_ref, bf16[128,4096]{1,0:T(8,128)(2,1)S(1)} %constant_dynamic-update-slice_fusion.src_ref, bf16[64,4096]{1,0:T(8,128)(2,1)S(1)} %broadcast_select_fusion.1.refs_0_, bf16[64,4096]{1,0:T(8,128)(2,1)S(1)} %broadcast_select_fusion.refs_1_), custom_call_target="tpu_custom_call" | custom-call | tf_op jit(solution)/shard_map/pallas_call | solution.py:68
  26.7 1.9 %collective-permute-start.7 = (f32[2,4096]{1,0:T(2,128)S(1)}, f32[2,4096]{1,0:T(2,128)S(1)}, u32[]{:S(2)}, u32[]{:S(2)}) collective-permute-start(f32[2,4096]{1,0:T(2,128)S(1)} %shard_map.40), channel_id=1, source_target_pairs={{0,16},{1,17},{2,18},{3,19},{4,20},{5,21},{6,22},{7,23},{8,24},{9,... | collective-permute-start | bytes 98312 | tf_op jit(solution)/shard_map/ppermute | solution.py:147
  28.6 2.1 %collective-permute-done.7 = f32[2,4096]{1,0:T(2,128)S(1)} collective-permute-done((f32[2,4096]{1,0:T(2,128)S(1)}, f32[2,4096]{1,0:T(2,128)S(1)}, u32[]{:S(2)}, u32[]{:S(2)}) %collective-permute-start.7) | collective-permute-done | bytes 32800 | tf_op jit(solution)/shard_map/ppermute | solution.py:147
  30.7 0.9 %collective-permute-start.8 = (f32[2,4096]{1,0:T(2,128)S(1)}, f32[2,4096]{1,0:T(2,128)S(1)}, u32[]{:S(2)}, u32[]{:S(2)}) collective-permute-start(f32[2,4096]{1,0:T(2,128)S(1)} %add.29), channel_id=1, source_target_pairs={{0,8},{1,9},{2,10},{3,11},{4,12},{5,13},{6,14},{7,15},{8,0},{9,1},... | collective-permute-start | bytes 98312 | tf_op jit(solution)/shard_map/ppermute | solution.py:147
  31.6 0.9 %collective-permute-done.8 = f32[2,4096]{1,0:T(2,128)S(1)} collective-permute-done((f32[2,4096]{1,0:T(2,128)S(1)}, f32[2,4096]{1,0:T(2,128)S(1)}, u32[]{:S(2)}, u32[]{:S(2)}) %collective-permute-start.8) | collective-permute-done | bytes 32800 | tf_op jit(solution)/shard_map/ppermute | solution.py:147
  32.5 0.6 %add_multiply_fusion = f32[2,4096]{1,0:T(2,128)} fusion(f32[2,4096]{1,0:T(2,128)S(1)} %add.29, f32[2,4096]{1,0:T(2,128)S(1)} %collective-permute-done.8), kind=kLoop, calls=%fused_computation.14 | loop fusion | flops 16384 | bytes 98304 | tf_op jit(solution)/shard_map/mul | solution.py:202
  (20 shorter events, 0.4 us)
Async XLA Ops:
  0.0 4.8 %collective-permute-start = (bf16[64,4096]{1,0:T(8,128)(2,1)}, bf16[64,4096]{1,0:T(8,128)(2,1)}, u32[]{:S(2)}, u32[]{:S(2)}) collective-permute-start(bf16[64,4096]{1,0:T(8,128)(2,1)} %refs_0_.1), channel_id=1, source_target_pairs={{0,8},{1,9},{2,10},{3,11},{4,12},{5,13},{6,14},{7,15},{8,0},{9,1},... | collective-permute-start | bytes 1572872 | tf_op jit(solution)/shard_map/ppermute | solution.py:147
  0.5 6.0 %collective-permute-start.2 = (bf16[64,4096]{1,0:T(8,128)(2,1)}, bf16[64,4096]{1,0:T(8,128)(2,1)S(1)}, u32[]{:S(2)}, u32[]{:S(2)}) collective-permute-start(bf16[64,4096]{1,0:T(8,128)(2,1)} %refs_1_.1), channel_id=1, source_target_pairs={{0,8},{1,9},{2,10},{3,11},{4,12},{5,13},{6,14},{7,15},{8,0},{9,1},... | collective-permute-start | bytes 1572872 | tf_op jit(solution)/shard_map/ppermute | solution.py:147
  0.5 10.4 %collective-permute-start.1 = (bf16[64,4096]{1,0:T(8,128)(2,1)}, bf16[64,4096]{1,0:T(8,128)(2,1)S(1)}, u32[]{:S(2)}, u32[]{:S(2)}) collective-permute-start(bf16[64,4096]{1,0:T(8,128)(2,1)} %refs_1_.1), channel_id=1, source_target_pairs={{0,1},{1,0},{2,3},{3,2},{4,5},{5,4},{6,7},{7,6},{8,24},{9,25},{10,... | collective-permute-start | bytes 1572872 | tf_op jit(solution)/shard_map/ppermute | solution.py:147
  6.5 4.8 %collective-permute-start.3 = (bf16[64,4096]{1,0:T(8,128)(2,1)S(1)}, bf16[64,4096]{1,0:T(8,128)(2,1)S(1)}, u32[]{:S(2)}, u32[]{:S(2)}) collective-permute-start(bf16[64,4096]{1,0:T(8,128)(2,1)S(1)} %collective-permute-done.2), channel_id=1, source_target_pairs={{8,24},{9,25},{10,26},{11,27},{12,28},{13,29},{14,30},{15,31},{24,... | collective-permute-start | bytes 1572872 | tf_op jit(solution)/shard_map/ppermute | solution.py:147
  11.5 5.4 %collective-permute-start.4 = (f16[136,256]{1,0:T(8,128)(2,1)S(1)}, f16[136,256]{1,0:T(8,128)(2,1)S(1)}, u32[]{:S(2)}, u32[]{:S(2)}) collective-permute-start(f16[136,256]{1,0:T(8,128)(2,1)S(1)} %pad_maximum_fusion.1), channel_id=1, source_target_pairs={{0,4},{1,5},{2,6},{3,7},{4,0},{5,1},{6,2},{7,3},{8,12},{9,13},{10,... | collective-permute-start | bytes 208904 | tf_op jit(solution)/shard_map/ppermute | solution.py:147
  17.1 4.4 %collective-permute-start.5 = (f16[136,256]{1,0:T(8,128)(2,1)S(1)}, f16[136,256]{1,0:T(8,128)(2,1)S(1)}, u32[]{:S(2)}, u32[]{:S(2)}) collective-permute-start(f16[136,256]{1,0:T(8,128)(2,1)S(1)} %pad_maximum_fusion.2), channel_id=1, source_target_pairs={{0,1},{1,0},{2,3},{3,2},{4,5},{5,4},{6,7},{7,6},{8,9},{9,8},{10,11... | collective-permute-start | bytes 208904 | tf_op jit(solution)/shard_map/ppermute | solution.py:147
  21.6 4.4 %collective-permute-start.6 = (f16[136,256]{1,0:T(8,128)(2,1)S(1)}, f16[136,256]{1,0:T(8,128)(2,1)S(1)}, u32[]{:S(2)}, u32[]{:S(2)}) collective-permute-start(f16[136,256]{1,0:T(8,128)(2,1)S(1)} %pad_maximum_fusion.3), channel_id=1, source_target_pairs={{0,2},{1,3},{2,0},{3,1},{4,6},{5,7},{6,4},{7,5},{8,10},{9,11},{10,... | collective-permute-start | bytes 208904 | tf_op jit(solution)/shard_map/ppermute | solution.py:147
  26.7 4.0 %collective-permute-start.7 = (f32[2,4096]{1,0:T(2,128)S(1)}, f32[2,4096]{1,0:T(2,128)S(1)}, u32[]{:S(2)}, u32[]{:S(2)}) collective-permute-start(f32[2,4096]{1,0:T(2,128)S(1)} %shard_map.40), channel_id=1, source_target_pairs={{0,16},{1,17},{2,18},{3,19},{4,20},{5,21},{6,22},{7,23},{8,24},{9,... | collective-permute-start | bytes 98312 | tf_op jit(solution)/shard_map/ppermute | solution.py:147
  30.7 1.7 %collective-permute-start.8 = (f32[2,4096]{1,0:T(2,128)S(1)}, f32[2,4096]{1,0:T(2,128)S(1)}, u32[]{:S(2)}, u32[]{:S(2)}) collective-permute-start(f32[2,4096]{1,0:T(2,128)S(1)} %add.29), channel_id=1, source_target_pairs={{0,8},{1,9},{2,10},{3,11},{4,12},{5,13},{6,14},{7,15},{8,0},{9,1},... | collective-permute-start | bytes 98312 | tf_op jit(solution)/shard_map/ppermute | solution.py:147

commit v6 on v5

--- a/solution.py
+++ b/solution.py
@@ -103,6 +103,36 @@
             out_ref[...] = jnp.dot(det_ref[...], weighted_ref[...], preferred_element_type=jnp.float32)
 
     return in_vmem(body, local.shape, local.dtype, local, det, weighted, flags=(local_first,))
+
+
+def finish_product(local_first, local, det, weighted, earlier):
+    rows, columns = earlier.shape
+    total_rows = rows + local.shape[0]
+
+    def body(flag, local_ref, det_ref, weighted_ref, earlier_ref, out_ref, exponent_ref):
+        out_ref[:rows, :] = earlier_ref[...]
+
+        @pl.when(flag[0] == 1)
+        def _():
+            out_ref[rows:, :] = local_ref[...]
+
+        @pl.when(flag[0] == 0)
+        def _():
+            out_ref[rows:, :] = jnp.dot(det_ref[...], weighted_ref[...], preferred_element_type=jnp.float32)
+
+        largest = jnp.max(jnp.abs(out_ref[...]), axis=0, keepdims=True)
+        exponent = jnp.ceil(jnp.log2(jnp.maximum(largest, SMALLEST)))
+        exponent_ref[...] = jnp.broadcast_to(exponent, exponent_ref.shape)
+
+    vmem = pl.BlockSpec(memory_space=pltpu.VMEM)
+    return pl.pallas_call(
+        body,
+        out_shape=[pltpu.VMEM((total_rows, columns), jnp.float32), pltpu.VMEM((TAG_ROWS, columns), jnp.float32)],
+        in_specs=[pl.BlockSpec(memory_space=pltpu.SMEM)] + [vmem] * 4,
+        out_specs=[vmem, vmem],
+        compiler_params=pltpu.CompilerParams(vmem_limit_bytes=16 << 20),
+        name="choose_product",
+    )(local_first, *(pltpu.with_memory_space_constraint(x, pltpu.VMEM) for x in (local, det, weighted, earlier)))
 
 
 def project(measured_b, src, dets, probe_count):
@@ -173,18 +203,25 @@
 
     flag = south.astype(jnp.int32).reshape(1)
     dets, products = [], []
-    for local, fetched in ((det_fields, fetched_a), (det_other, fetched_b)):
+    for label, local, fetched in (("a", det_fields, fetched_a), ("b", det_other, fetched_b)):
         local_product = measure(local)
         for j, block in enumerate(fetched):
             if j:
                 dets.append(block)
                 products.append(measure(block))
+                exponent = None
             else:
                 dets.append(jnp.where(south, local, block))
-                products.append(choose_product(flag, local_product, block, weighted))
-    measured = jnp.concatenate(products, axis=0)
-
-    exponent = jnp.ceil(jnp.log2(jnp.maximum(jnp.max(jnp.abs(measured), axis=0, keepdims=True), SMALLEST)))
+                if label == "b":
+                    earlier = products[0] if len(products) == 1 else jnp.concatenate(products, axis=0)
+                    measured, exponent = finish_product(flag, local_product, block, weighted, earlier)
+                    exponent, products = exponent[:1], [measured]
+                else:
+                    products.append(choose_product(flag, local_product, block, weighted))
+    measured = products[0] if len(products) == 1 else jnp.concatenate(products, axis=0)
+
+    if exponent is None:
+        exponent = jnp.ceil(jnp.log2(jnp.maximum(jnp.max(jnp.abs(measured), axis=0, keepdims=True), SMALLEST)))
     widths = [1 << i for i in range(slabs.bit_length() - 1)]
     for width in widths[-1:] + widths[:-1]:
         sent = exchange(pack(measured, exponent), lambda q, c, u, width=width: (q, c, u ^ width))

time: 33.3 us -> 33.9 us (1.018)
  starting transfers between devices: 14 us -> 14.8 us
    ppermute x9, starting transfers between devices: 14 us -> 14.8 us  [exchange(): return lax.ppermute(array, ('blk', 'vox'), pairs)]
    pallas_call x4 -> x3, Pallas kernels: 1.38 us -> 1.36 us  [in_vmem(): pl.pallas_call(body, out_shape=pltpu.VMEM(shape, dtype), in_specs=[pl.Blo...]
  transfers between devices with their start and end apart: 9 -> 9, of which waited for: 6 -> 6; matrix products, arithmetic and copies ran while one was open for 7% -> 6% of each run, Pallas kernels for 6% -> 6%
where the time goes in v6:
time: 33.9 us; the launch traced here: 33.7 us
  starting transfers between devices  14.8 us (44%)
  waiting for transfers between devices  13 us (38%)
  Pallas kernels  2.62 us (8%)
  local copies, waits for them, and re-layouts  1.14 us (3%)
  other arithmetic  1.09 us (3%)
  matrix products  0.94 us (3%)
    ppermute x9, starting transfers between devices, exchange(): return lax.ppermute(array, ('blk', 'vox'), pairs)  14.8 us
    ppermute x9, waiting for transfers between devices, exchange(): return lax.ppermute(array, ('blk', 'vox'), pairs)  13 us
    pallas_call x3, Pallas kernels, in_vmem(): pl.pallas_call(body, out_shape=pltpu.VMEM(shape, dtype), in_specs=[pl.Blo...  1.36 us
    pallas_call x1, Pallas kernels, stage(): pl.pallas_call(body, out_shape=[pltpu.VMEM(a.shape, a.dtype) for a in arr...  1.23 us
    concatenate x1, local copies, waits for them, and re-layouts, product(): src = jnp.concatenate([src_fields, src_other], axis=0)  1.08 us
    dot_general x2, matrix products, measure(): return jnp.dot(det, weighted, preferred_element_type=jnp.float32)  0.94 us
  transfers between devices with their start and end apart: 9, of which 6 were waited for; matrix products, arithmetic and copies ran while one was open for 6% of the time, Pallas kernels for 6%

profile of v6, /device:TPU:0, one launch (start us, length us, event | category | flops | bytes accessed | tf_op | source)
XLA Modules:
  0.0 33.7 jit_solution(9402602191432430828)
XLA Ops:
  0.0 0.5 %collective-permute-start = (bf16[64,4096]{1,0:T(8,128)(2,1)}, bf16[64,4096]{1,0:T(8,128)(2,1)}, u32[]{:S(2)}, u32[]{:S(2)}) collective-permute-start(bf16[64,4096]{1,0:T(8,128)(2,1)} %refs_0_.1), channel_id=1, source_target_pairs={{0,8},{1,9},{2,10},{3,11},{4,12},{5,13},{6,14},{7,15},{8,0},{9,1},... | collective-permute-start | bytes 1572872 | tf_op jit(solution)/shard_map/ppermute | solution.py:177
  0.5 2.5 %collective-permute-start.3 = (bf16[64,4096]{1,0:T(8,128)(2,1)}, bf16[64,4096]{1,0:T(8,128)(2,1)S(1)}, u32[]{:S(2)}, u32[]{:S(2)}) collective-permute-start(bf16[64,4096]{1,0:T(8,128)(2,1)} %refs_1_.1), channel_id=1, source_target_pairs={{0,1},{1,0},{2,3},{3,2},{4,5},{5,4},{6,7},{7,6},{8,24},{9,25},{10,... | collective-permute-start | bytes 1572872 | tf_op jit(solution)/shard_map/ppermute | solution.py:177
  3.0 0.2 collective-permute-start.1
  3.2 1.2 %stage.1 = (bf16[64,4096]{1,0:T(8,128)(2,1)S(1)}, bf16[64,4096]{1,0:T(8,128)(2,1)S(1)}, bf16[2,4096]{1,0:T(2,128)(2,1)S(1)}) custom-call(bf16[64,4096]{1,0:T(8,128)(2,1)} %refs_0_.1, bf16[64,4096]{1,0:T(8,128)(2,1)} %refs_1_.1, bf16[2,4096]{1,0:T(2,128)(2,1)} %refs_2_.1), custom_call_target="tpu_custom_call" | custom-call | tf_op jit(solution)/shard_map/stage/pallas_call | solution.py:56
  4.5 0.0 collective-permute-done
  4.5 1.1 %constant_dynamic-update-slice_fusion.src_ref = bf16[128,4096]{1,0:T(8,128)(2,1)S(1)} fusion(bf16[128,4096]{1,0:T(8,128)(2,1)S(1)} %constant_dynamic-update-slice_fusion.1, bf16[64,4096]{1,0:T(8,128)(2,1)} %collective-permute-done), kind=kLoop, calls=%fused_computation.13 | loop fusion | bytes 1048576 | tf_op jit(solution)/shard_map/concatenate | solution.py:198
  5.6 0.6 %shard_map.37.weighted_ref = bf16[4096,256]{1,0:T(8,128)(2,1)S(1)} custom-call(bf16[128,4096]{1,0:T(8,128)(2,1)S(1)} %constant_dynamic-update-slice_fusion.src_ref, bf16[2,4096]{1,0:T(2,128)(2,1)S(1)} %get-tuple-element.11.probes_ref), custom_call_target="tpu_custom_call" | custom-call | tf_op jit(solution)/shard_map/pallas_call | solution.py:68
  6.2 0.0 collective-permute-done.1
  6.2 0.7 %collective-permute-start.2 = (bf16[64,4096]{1,0:T(8,128)(2,1)S(1)}, bf16[64,4096]{1,0:T(8,128)(2,1)S(1)}, u32[]{:S(2)}, u32[]{:S(2)}) collective-permute-start(bf16[64,4096]{1,0:T(8,128)(2,1)S(1)} %collective-permute-done.1), channel_id=1, source_target_pairs={{8,24},{9,25},{10,26},{11,27},{12,28},{13,29},{14,30},{15,31},{24,... | collective-permute-start | bytes 1572872 | tf_op jit(solution)/shard_map/ppermute | solution.py:177
  6.9 0.5 %fusion.3.local_ref = f32[64,256]{1,0:T(8,128)S(1)} fusion(bf16[64,4096]{1,0:T(8,128)(2,1)S(1)} %get-tuple-element.12, bf16[4096,256]{1,0:T(8,128)(2,1)S(1)} %shard_map.37.weighted_ref), kind=kOutput, calls=%fused_computation.31 | convolution fusion | flops 134217728 | bytes 2686976 | tf_op jit(solution)/shard_map/dot_general | solution.py:202
  7.4 3.0 %collective-permute-done.3.det_ref = bf16[64,4096]{1,0:T(8,128)(2,1)S(1)} collective-permute-done((bf16[64,4096]{1,0:T(8,128)(2,1)}, bf16[64,4096]{1,0:T(8,128)(2,1)S(1)}, u32[]{:S(2)}, u32[]{:S(2)}) %collective-permute-start.3) | collective-permute-done | bytes 524320 | tf_op jit(solution)/shard_map/ppermute | solution.py:177
  10.4 0.5 %convolution_bitcast_fusion.local_ref = f32[64,256]{1,0:T(8,128)S(1)} fusion(bf16[64,4096]{1,0:T(8,128)(2,1)S(1)} %collective-permute-done.1, bf16[4096,256]{1,0:T(8,128)(2,1)S(1)} %shard_map.37.weighted_ref), kind=kOutput, calls=%fused_computation | convolution fusion | flops 134217728 | bytes 2686976 | tf_op jit(solution)/shard_map/dot_general | solution.py:202
  10.8 0.0 collective-permute-done.2.det_ref
  11.0 3.2 %collective-permute-start.4 = (f16[136,256]{1,0:T(8,128)(2,1)S(1)}, f16[136,256]{1,0:T(8,128)(2,1)S(1)}, u32[]{:S(2)}, u32[]{:S(2)}) collective-permute-start(f16[136,256]{1,0:T(8,128)(2,1)S(1)} %pad_maximum_fusion), channel_id=1, source_target_pairs={{0,4},{1,5},{2,6},{3,7},{4,0},{5,1},{6,2},{7,3},{8,12},{9,13},{10,... | collective-permute-start | bytes 208904 | tf_op jit(solution)/shard_map/ppermute | solution.py:177
  14.2 2.3 %collective-permute-done.4 = f16[136,256]{1,0:T(8,128)(2,1)S(1)} collective-permute-done((f16[136,256]{1,0:T(8,128)(2,1)S(1)}, f16[136,256]{1,0:T(8,128)(2,1)S(1)}, u32[]{:S(2)}, u32[]{:S(2)}) %collective-permute-start.4) | collective-permute-done | bytes 69664 | tf_op jit(solution)/shard_map/ppermute | solution.py:177
  16.6 1.9 %collective-permute-start.5 = (f16[136,256]{1,0:T(8,128)(2,1)S(1)}, f16[136,256]{1,0:T(8,128)(2,1)S(1)}, u32[]{:S(2)}, u32[]{:S(2)}) collective-permute-start(f16[136,256]{1,0:T(8,128)(2,1)S(1)} %pad_maximum_fusion.1), channel_id=1, source_target_pairs={{0,1},{1,0},{2,3},{3,2},{4,5},{5,4},{6,7},{7,6},{8,9},{9,8},{10,11... | collective-permute-start | bytes 208904 | tf_op jit(solution)/shard_map/ppermute | solution.py:177
  18.5 0.1 broadcast_select_fusion.1.refs_0_
  18.5 2.4 %collective-permute-done.5 = f16[136,256]{1,0:T(8,128)(2,1)S(1)} collective-permute-done((f16[136,256]{1,0:T(8,128)(2,1)S(1)}, f16[136,256]{1,0:T(8,128)(2,1)S(1)}, u32[]{:S(2)}, u32[]{:S(2)}) %collective-permute-start.5) | collective-permute-done | bytes 69664 | tf_op jit(solution)/shard_map/ppermute | solution.py:177
  21.1 2.0 %collective-permute-start.6 = (f16[136,256]{1,0:T(8,128)(2,1)S(1)}, f16[136,256]{1,0:T(8,128)(2,1)S(1)}, u32[]{:S(2)}, u32[]{:S(2)}) collective-permute-start(f16[136,256]{1,0:T(8,128)(2,1)S(1)} %pad_maximum_fusion.2), channel_id=1, source_target_pairs={{0,2},{1,3},{2,0},{3,1},{4,6},{5,7},{6,4},{7,5},{8,10},{9,11},{10,... | collective-permute-start | bytes 208904 | tf_op jit(solution)/shard_map/ppermute | solution.py:177
  23.0 0.1 broadcast_select_fusion.refs_1_
  23.1 2.3 %collective-permute-done.6 = f16[136,256]{1,0:T(8,128)(2,1)S(1)} collective-permute-done((f16[136,256]{1,0:T(8,128)(2,1)S(1)}, f16[136,256]{1,0:T(8,128)(2,1)S(1)}, u32[]{:S(2)}, u32[]{:S(2)}) %collective-permute-start.6) | collective-permute-done | bytes 69664 | tf_op jit(solution)/shard_map/ppermute | solution.py:177
  25.5 0.1 add_convert_fusion.measured_ref
  25.5 0.7 %shard_map.39 = f32[2,4096]{1,0:T(2,128)S(1)} custom-call(bf16[128,256]{1,0:T(8,128)(2,1)S(1)} %add_convert_fusion.measured_ref, bf16[128,4096]{1,0:T(8,128)(2,1)S(1)} %constant_dynamic-update-slice_fusion.src_ref, bf16[64,4096]{1,0:T(8,128)(2,1)S(1)} %broadcast_select_fusion.1.refs_0_, bf16[64,4096]{1,0:T(8,128)(2,1)S(1)} %broadcast_select_fusion.refs_1_), custom_call_target="tpu_custom_call" | custom-call | tf_op jit(solution)/shard_map/pallas_call | solution.py:68
  26.2 1.9 %collective-permute-start.7 = (f32[2,4096]{1,0:T(2,128)S(1)}, f32[2,4096]{1,0:T(2,128)S(1)}, u32[]{:S(2)}, u32[]{:S(2)}) collective-permute-start(f32[2,4096]{1,0:T(2,128)S(1)} %shard_map.39), channel_id=1, source_target_pairs={{0,16},{1,17},{2,18},{3,19},{4,20},{5,21},{6,22},{7,23},{8,24},{9,... | collective-permute-start | bytes 98312 | tf_op jit(solution)/shard_map/ppermute | solution.py:177
  28.1 2.1 %collective-permute-done.7 = f32[2,4096]{1,0:T(2,128)S(1)} collective-permute-done((f32[2,4096]{1,0:T(2,128)S(1)}, f32[2,4096]{1,0:T(2,128)S(1)}, u32[]{:S(2)}, u32[]{:S(2)}) %collective-permute-start.7) | collective-permute-done | bytes 32800 | tf_op jit(solution)/shard_map/ppermute | solution.py:177
  30.2 1.9 %collective-permute-start.8 = (f32[2,4096]{1,0:T(2,128)S(1)}, f32[2,4096]{1,0:T(2,128)S(1)}, u32[]{:S(2)}, u32[]{:S(2)}) collective-permute-start(f32[2,4096]{1,0:T(2,128)S(1)} %add.29), channel_id=1, source_target_pairs={{0,8},{1,9},{2,10},{3,11},{4,12},{5,13},{6,14},{7,15},{8,0},{9,1},... | collective-permute-start | bytes 98312 | tf_op jit(solution)/shard_map/ppermute | solution.py:177
  32.2 0.9 %collective-permute-done.8 = f32[2,4096]{1,0:T(2,128)S(1)} collective-permute-done((f32[2,4096]{1,0:T(2,128)S(1)}, f32[2,4096]{1,0:T(2,128)S(1)}, u32[]{:S(2)}, u32[]{:S(2)}) %collective-permute-start.8) | collective-permute-done | bytes 32800 | tf_op jit(solution)/shard_map/ppermute | solution.py:177
  33.0 0.6 %add_multiply_fusion = f32[2,4096]{1,0:T(2,128)} fusion(f32[2,4096]{1,0:T(2,128)S(1)} %add.29, f32[2,4096]{1,0:T(2,128)S(1)} %collective-permute-done.8), kind=kLoop, calls=%fused_computation.12 | loop fusion | flops 16384 | bytes 98304 | tf_op jit(solution)/shard_map/mul | solution.py:239
  (20 shorter events, 0.4 us)
Async XLA Ops:
  0.0 4.5 %collective-permute-start = (bf16[64,4096]{1,0:T(8,128)(2,1)}, bf16[64,4096]{1,0:T(8,128)(2,1)}, u32[]{:S(2)}, u32[]{:S(2)}) collective-permute-start(bf16[64,4096]{1,0:T(8,128)(2,1)} %refs_0_.1), channel_id=1, source_target_pairs={{0,8},{1,9},{2,10},{3,11},{4,12},{5,13},{6,14},{7,15},{8,0},{9,1},... | collective-permute-start | bytes 1572872 | tf_op jit(solution)/shard_map/ppermute | solution.py:177
  0.5 9.9 %collective-permute-start.3 = (bf16[64,4096]{1,0:T(8,128)(2,1)}, bf16[64,4096]{1,0:T(8,128)(2,1)S(1)}, u32[]{:S(2)}, u32[]{:S(2)}) collective-permute-start(bf16[64,4096]{1,0:T(8,128)(2,1)} %refs_1_.1), channel_id=1, source_target_pairs={{0,1},{1,0},{2,3},{3,2},{4,5},{5,4},{6,7},{7,6},{8,24},{9,25},{10,... | collective-permute-start | bytes 1572872 | tf_op jit(solution)/shard_map/ppermute | solution.py:177
  3.0 3.2 %collective-permute-start.1 = (bf16[64,4096]{1,0:T(8,128)(2,1)}, bf16[64,4096]{1,0:T(8,128)(2,1)S(1)}, u32[]{:S(2)}, u32[]{:S(2)}) collective-permute-start(bf16[64,4096]{1,0:T(8,128)(2,1)} %refs_1_.1), channel_id=1, source_target_pairs={{0,8},{1,9},{2,10},{3,11},{4,12},{5,13},{6,14},{7,15},{8,0},{9,1},... | collective-permute-start | bytes 1572872 | tf_op jit(solution)/shard_map/ppermute | solution.py:177
  6.2 4.6 %collective-permute-start.2 = (bf16[64,4096]{1,0:T(8,128)(2,1)S(1)}, bf16[64,4096]{1,0:T(8,128)(2,1)S(1)}, u32[]{:S(2)}, u32[]{:S(2)}) collective-permute-start(bf16[64,4096]{1,0:T(8,128)(2,1)S(1)} %collective-permute-done.1), channel_id=1, source_target_pairs={{8,24},{9,25},{10,26},{11,27},{12,28},{13,29},{14,30},{15,31},{24,... | collective-permute-start | bytes 1572872 | tf_op jit(solution)/shard_map/ppermute | solution.py:177
  11.0 5.4 %collective-permute-start.4 = (f16[136,256]{1,0:T(8,128)(2,1)S(1)}, f16[136,256]{1,0:T(8,128)(2,1)S(1)}, u32[]{:S(2)}, u32[]{:S(2)}) collective-permute-start(f16[136,256]{1,0:T(8,128)(2,1)S(1)} %pad_maximum_fusion), channel_id=1, source_target_pairs={{0,4},{1,5},{2,6},{3,7},{4,0},{5,1},{6,2},{7,3},{8,12},{9,13},{10,... | collective-permute-start | bytes 208904 | tf_op jit(solution)/shard_map/ppermute | solution.py:177
  16.6 4.4 %collective-permute-start.5 = (f16[136,256]{1,0:T(8,128)(2,1)S(1)}, f16[136,256]{1,0:T(8,128)(2,1)S(1)}, u32[]{:S(2)}, u32[]{:S(2)}) collective-permute-start(f16[136,256]{1,0:T(8,128)(2,1)S(1)} %pad_maximum_fusion.1), channel_id=1, source_target_pairs={{0,1},{1,0},{2,3},{3,2},{4,5},{5,4},{6,7},{7,6},{8,9},{9,8},{10,11... | collective-permute-start | bytes 208904 | tf_op jit(solution)/shard_map/ppermute | solution.py:177
  21.1 4.4 %collective-permute-start.6 = (f16[136,256]{1,0:T(8,128)(2,1)S(1)}, f16[136,256]{1,0:T(8,128)(2,1)S(1)}, u32[]{:S(2)}, u32[]{:S(2)}) collective-permute-start(f16[136,256]{1,0:T(8,128)(2,1)S(1)} %pad_maximum_fusion.2), channel_id=1, source_target_pairs={{0,2},{1,3},{2,0},{3,1},{4,6},{5,7},{6,4},{7,5},{8,10},{9,11},{10,... | collective-permute-start | bytes 208904 | tf_op jit(solution)/shard_map/ppermute | solution.py:177
  26.2 4.0 %collective-permute-start.7 = (f32[2,4096]{1,0:T(2,128)S(1)}, f32[2,4096]{1,0:T(2,128)S(1)}, u32[]{:S(2)}, u32[]{:S(2)}) collective-permute-start(f32[2,4096]{1,0:T(2,128)S(1)} %shard_map.39), channel_id=1, source_target_pairs={{0,16},{1,17},{2,18},{3,19},{4,20},{5,21},{6,22},{7,23},{8,24},{9,... | collective-permute-start | bytes 98312 | tf_op jit(solution)/shard_map/ppermute | solution.py:177
  30.2 2.8 %collective-permute-start.8 = (f32[2,4096]{1,0:T(2,128)S(1)}, f32[2,4096]{1,0:T(2,128)S(1)}, u32[]{:S(2)}, u32[]{:S(2)}) collective-permute-start(f32[2,4096]{1,0:T(2,128)S(1)} %add.29), channel_id=1, source_target_pairs={{0,8},{1,9},{2,10},{3,11},{4,12},{5,13},{6,14},{7,15},{8,0},{9,1},... | collective-permute-start | bytes 98312 | tf_op jit(solution)/shard_map/ppermute | solution.py:177
